TPU v7x, 256 devices: a whole 4x4x8 slice. The times are simulated.
256 devices in a mesh: lon: 16 (over x, y), lat: 16 (over z, core).
Axes of the slice: x: 4, y: 4, z: 8, core: 2. Of those that a mesh axis runs over, the one named last changes fastest.
Arguments:
- meridional_speed: float32 [16, 1024, 4096], P(None, 'lat', 'lon'), may hold values from -6 to 6
- theta_field: float32 [16, 1024, 4096], P(None, 'lat', 'lon'), may hold values from -2 to 30
- tier_vertical_span: float32 [16], replicated, may hold values from 0.5 to 4
- grid_zonal_span: float32 [1024, 4096], P('lat', 'lon'), may hold values from 0.05 to 40
- grid_plan_extent: float32 [1024, 4096], P('lat', 'lon'), may hold values from 0.2 to 5
- ocean_energy_input: float32 [1024, 4096], P('lat', 'lon'), may hold values from -6 to 6
- ocean_tier_tally: int32 [1024, 4096], P('lat', 'lon'), may hold values from 0 to 16, as said below
- grid_region_label: int32 [1024, 4096], P('lat', 'lon'), may hold values from 0 to 3
- seam_matching_meridian: int32 [4096], P('lon'), may hold values from 0 to 4095, as said below
Outputs:
- class_transport: float32 [4, 1024, 128], P(None, 'lat')
- overturning: float32 [4, 1024, 16], P(None, 'lat')
- heat_transport: float32 [4, 1024], P(None, 'lat')
- implied_transport: float32 [4, 1024], P(None, 'lat')
Inputs may be any that keep to these rules, and one draw needn't show every extreme that they name: `ocean_tier_tally`: one column, the same at every latitude, has at least one wet level, and every column of the northernmost row has at least one. seam_matching_meridian[i] = (c - i) mod 4096 for a c that each draw picks.
All inputs are finite; a program needn't handle non-finite values.
Results may differ from a plain program's by a relative error of at most 0.0003.
Values sent between devices are 32-bit elements; how exact they have to be, the bound alone decides.
No kernel may reach another device: no remote copies, remote signals or barrier semaphores. Data moves between devices by JAX's collectives and lax.ppermute only.
A program may use at most 64 MiB of HBM per device.

v0:
```python
import math

import jax
import jax.numpy as jnp
from jax import lax
from jax.sharding import PartitionSpec as P

THERMAL_BINS = 128
OCEAN_REGIONS = 4


THERMAL_FLOOR = -2.0
THERMAL_RANGE = 32.0


def copy_for_each(array, axis):
    copies = jnp.broadcast_to(array, (lax.axis_size(axis), *array.shape))
    return lax.all_to_all(copies, axis, split_axis=0, concat_axis=0, tiled=True)


def folded_in_pairs(pieces, combine):
    while len(jax.tree.leaves(pieces)[0]) > 1:
        pieces = jax.vmap(combine)(*(pieces[side::2] for side in (0, 1)))
    return pieces[0]


def prefix(array, axis, combine, identity):
    devices, index = (lax.axis_size(axis), lax.axis_index(axis))
    passed = jnp.arange(devices) < index

    def kept(part, zero, own):
        part = jnp.where(
            passed.reshape(-1, *(1 for _ in own.shape)), part, jnp.asarray(zero, own.dtype)
        )
        return part

    pieces = copy_for_each(array, axis)
    return folded_in_pairs(kept(pieces, identity, array), combine)


def passed_along(block, axis, distance):
    devices = range(lax.axis_size(axis))
    route = [(i - distance, i) for i in devices if i - distance in devices]
    return lax.ppermute(block, axis, route)


def in_order(parts, dim):
    parts = jnp.moveaxis(parts, 0, dim)
    dims = parts.shape
    return parts.reshape(*dims[:dim], dims[dim] * dims[dim + 1], *dims[dim + 2 :])


def gathered_copies(array, axis, dim):
    return in_order(copy_for_each(array, axis), dim)


def taken_together(array, axis):
    everything = copy_for_each(array, axis)
    return jnp.sum(everything, axis=0)


def packed_total(arrays, axis):
    ends = [0]
    for a in arrays:
        ends.append(ends[-1] + a.size)
    so_far = taken_together(jnp.concatenate([a.ravel() for a in arrays]), axis)
    return tuple((so_far[b:e].reshape(a.shape) for a, b, e in zip(arrays, ends, ends[1:])))


def theta_bucket_edges(
    mass_conveyance, bucket_membership, lower_real_value, upper_interp_factor, theta_bucket_tally
):
    tier_ordinal, parallel_tally, meridian_tally = mass_conveyance.shape
    region_tally = bucket_membership.shape[0]
    block_rows = math.gcd(parallel_tally, 8)
    blocks = parallel_tally // block_rows

    def split_rows(array):
        lead = array.shape[0]
        return jnp.transpose(array.reshape(lead, blocks, block_rows, meridian_tally), (1, 0, 2, 3))

    def one_block(pieces):
        trans_blk, member_blk, low_blk, weight_blk = pieces
        theta_buckets = lax.broadcasted_iota(jnp.int32, (1, 1, 1, theta_bucket_tally), 3).astype(
            jnp.float32
        )
        low_cols = low_blk[..., None]
        weight_cols = weight_blk[..., None]
        tent = jnp.where(theta_buckets == low_cols, 1.0 - weight_cols, 0.0) + jnp.where(
            theta_buckets == low_cols + 1.0, weight_cols, 0.0
        )
        weighted = member_blk[:, None, :, :] * trans_blk[None, :, :, :]
        return jnp.einsum("bkri,krim->brm", weighted, tent, precision=lax.Precision.HIGHEST)

    binned = lax.map(
        one_block,
        (
            split_rows(mass_conveyance),
            split_rows(bucket_membership),
            split_rows(lower_real_value),
            split_rows(upper_interp_factor),
        ),
    )
    return jnp.transpose(binned, (1, 0, 2, 3)).reshape(
        region_tally, parallel_tally, theta_bucket_tally
    )


def vertical_aggregate_field(
    meridional_speed,
    theta_field,
    tier_vertical_span,
    grid_zonal_span,
    grid_plan_extent,
    ocean_energy_input,
    ocean_tier_tally,
    grid_region_label,
    subsequent_theta,
    subsequent_vertical_extent,
    theta_bucket_tally,
    region_tally,
):
    tier_ordinal, parallel_tally, meridian_tally = theta_field.shape
    poleward_theta = jnp.concatenate([theta_field[:, 1:, :], subsequent_theta[:, None, :]], axis=1)
    interface_theta = 0.5 * (theta_field + poleward_theta)
    north_depth = jnp.concatenate(
        [ocean_tier_tally[1:, :], subsequent_vertical_extent[None, :]], axis=0
    )
    face_depth = jnp.minimum(ocean_tier_tally, north_depth)
    level_iota = lax.broadcasted_iota(jnp.int32, (tier_ordinal, 1, 1), 0)
    wet_mask = (level_iota < face_depth[None, :, :]).astype(jnp.float32)
    water_capacity = wet_mask * tier_vertical_span[:, None, None] * grid_zonal_span[None, :, :]
    mass_conveyance = water_capacity * meridional_speed
    bucket_spacing = THERMAL_RANGE / theta_bucket_tally
    placement_offset = jnp.clip(
        (interface_theta - THERMAL_FLOOR) / bucket_spacing, 0.0, theta_bucket_tally - 1.0
    )
    lower_real_value = jnp.minimum(jnp.floor(placement_offset), theta_bucket_tally - 2.0)
    upper_interp_factor = placement_offset - lower_real_value
    basin_iota = lax.broadcasted_iota(jnp.int32, (region_tally, 1, 1), 0)
    bucket_membership = (grid_region_label[None, :, :] == basin_iota).astype(jnp.float32)
    bucket_aggregate = theta_bucket_edges(
        mass_conveyance,
        bucket_membership,
        lower_real_value,
        upper_interp_factor,
        theta_bucket_tally,
    )
    level_sum = jnp.einsum(
        "bji,kji->bjk", bucket_membership, mass_conveyance, precision=lax.Precision.HIGHEST
    )
    energy_aggregate = jnp.einsum(
        "dwk,wk->dw",
        bucket_membership,
        jnp.sum(mass_conveyance * interface_theta, axis=0),
        precision=lax.Precision.HIGHEST,
    )
    parallel_theta_field = jnp.sum(water_capacity * interface_theta, axis=(0, 2))
    row_wet = jnp.sum(water_capacity, axis=(0, 2))
    flux_rows = jnp.einsum(
        "dwk,wk->dw",
        bucket_membership,
        ocean_energy_input * grid_plan_extent,
        precision=lax.Precision.HIGHEST,
    )
    return (bucket_aggregate, level_sum, energy_aggregate, parallel_theta_field, row_wet, flux_rows)


def finish_rows(
    bucket_aggregate, level_sum, energy_aggregate, parallel_theta_field, row_wet, unit_scale
):
    row_mean = parallel_theta_field / row_wet
    volume_total = jnp.sum(level_sum, axis=2)
    heat_out = unit_scale / 16.0 * (energy_aggregate - volume_total * row_mean[None, :])
    stream = unit_scale * jnp.cumsum(level_sum, axis=2)
    return (unit_scale * bucket_aggregate, stream, heat_out)


def combine_sum(earlier, later):
    return earlier + later


def south_offset(totals):
    return prefix(totals, "lat", combine_sum, jnp.zeros_like(totals))


def body(
    meridional_speed,
    theta_field,
    tier_vertical_span,
    grid_zonal_span,
    grid_plan_extent,
    ocean_energy_input,
    ocean_tier_tally,
    grid_region_label,
    seam_matching_meridian,
):
    tier_ordinal, parallel_tally, meridian_tally = theta_field.shape
    lon_size = lax.axis_size("lon")
    lat_size = lax.axis_size("lat")
    width_total = meridian_tally * lon_size
    height_total = parallel_tally * lat_size
    unit_scale = math.sqrt(THERMAL_BINS / (width_total * tier_ordinal))
    implied_scale = 2.0 / math.sqrt(width_total * height_total)
    equatorward_limit_value = (theta_field[:, 0, :], ocean_tier_tally[0, :].astype(jnp.float32))
    upper_theta_value, above_depth = passed_along(
        (equatorward_limit_value[0], equatorward_limit_value[1]), "lat", -1
    )
    fold_edge = (
        theta_field[:, parallel_tally - 1, :],
        ocean_tier_tally[parallel_tally - 1, :].astype(jnp.float32),
    )
    seam_theta, fold_depth = (
        gathered_copies(fold_edge[0], "lon", 1),
        gathered_copies(fold_edge[1], "lon", 0),
    )
    reflected_theta = jnp.take(seam_theta, seam_matching_meridian, axis=1)
    mirror_depth = jnp.take(fold_depth, seam_matching_meridian, axis=0)
    on_seam_flag = lax.axis_index("lat") == lat_size - 1
    subsequent_theta = jnp.where(on_seam_flag, reflected_theta, upper_theta_value)
    subsequent_vertical_extent = jnp.where(on_seam_flag, mirror_depth, above_depth).astype(
        jnp.int32
    )
    bucket_aggregate, level_sum, energy_aggregate, parallel_theta_field, row_wet, flux_rows = (
        vertical_aggregate_field(
            meridional_speed,
            theta_field,
            tier_vertical_span,
            grid_zonal_span,
            grid_plan_extent,
            ocean_energy_input,
            ocean_tier_tally,
            grid_region_label,
            subsequent_theta,
            subsequent_vertical_extent,
            THERMAL_BINS,
            OCEAN_REGIONS,
        )
    )
    summed = packed_total(
        (bucket_aggregate, level_sum, energy_aggregate, parallel_theta_field, row_wet, flux_rows),
        "lon",
    )
    class_out, stream, heat_out = finish_rows(
        summed[0], summed[1], summed[2], summed[3], summed[4], unit_scale
    )
    flux_total = summed[5]
    late_offset = south_offset(jnp.sum(flux_total, axis=1))
    implied = implied_scale * (late_offset[:, None] + jnp.cumsum(flux_total, axis=1))
    return (class_out, stream, heat_out, implied)


def solution(mesh):
    in_specs = (
        P(None, "lat", "lon"),
        P(None, "lat", "lon"),
        P(),
        P("lat", "lon"),
        P("lat", "lon"),
        P("lat", "lon"),
        P("lat", "lon"),
        P("lat", "lon"),
        P("lon"),
    )
    out_specs = (P(None, "lat", None), P(None, "lat", None), P(None, "lat"), P(None, "lat"))
    return jax.shard_map(body, mesh=mesh, in_specs=in_specs, out_specs=out_specs, check_vma=False)
```

profile of v0, /device:TPU:32, one launch (start us, length us, event | category | flops | bytes accessed | tf_op | source)
XLA Modules:
  0.0 319.4 jit_solution(11539599296509700534)
XLA Ops:
  0.6 0.7 slice_convert_fusion.1
  1.4 1.9 collective-permute-start.1
  3.3 0.6 broadcast_in_dim.90
  3.9 7.0 %all-to-all-start.1 = ((f32[16,1,256]{2,1,0:T(1,128)}), f32[16,1,256]{2,1,0:T(1,128)S(1)}, u32[]{:S(2)}, u32[]{:S(2)}) async-start(f32[16,1,256]{2,1,0:T(1,128)} %broadcast_in_dim.90), calls=%async_computation.1 | async-start | bytes 32768 | tf_op jit(solution)/shard_map/all_to_all | solution.py:18
  10.9 1.0 fusion.35
  12.0 1.9 collective-permute-start
  14.0 0.7 compare_select_fusion
  14.6 0.9 multiply_bitcast_fusion
  15.6 1.3 fusion.23
  16.9 0.9 fusion.25
  17.8 0.8 slice.81
  18.6 1.3 slice.78
  20.1 0.7 reshape.126
  20.7 0.7 broadcast_in_dim.86
  21.4 7.3 %all-to-all-start = ((f32[16,16,256]{2,1,0:T(8,128)}), f32[16,16,256]{2,1,0:T(8,128)S(1)}, u32[]{:S(2)}, u32[]{:S(2)}) async-start(f32[16,16,256]{2,1,0:T(8,128)} %broadcast_in_dim.86), calls=%async_computation | async-start | bytes 524288 | tf_op jit(solution)/shard_map/all_to_all | solution.py:18
  28.8 1.7 gather_fusion.1
  30.6 7.4 %all-to-all-done = f32[16,16,256]{2,1,0:T(8,128)S(1)} async-done(((f32[16,16,256]{2,1,0:T(8,128)}), f32[16,16,256]{2,1,0:T(8,128)S(1)}, u32[]{:S(2)}, u32[]{:S(2)}) %all-to-all-start) | async-done | bytes 262176 | tf_op jit(solution)/shard_map/all_to_all | solution.py:18
  38.0 2.0 copy.57
  39.9 2.3 gather_fusion
  42.4 2.4 multiply_reduce_fusion
  44.9 1.2 convolution_bitcast_fusion
  46.1 0.6 copy.62
  47.2 0.7 reshape.125
  47.8 0.7 reshape.124
  48.9 0.6 copy.61
  49.5 0.6 copy.60
  50.1 208.4 %while.10 = (s32[]{:T(128)}, f32[8,4,8,128]{3,2,0,1:T(8,128)S(1)}, f32[8,16,8,256]{3,1,2,0:T(8,128)S(1)}, f32[8,16,8,256]{3,1,2,0:T(8,128)S(1)}, f32[8,4,8,256]{...) while((s32[]{:T(128)}, f32[8,4,8,128]{3,2,0,1:T(8,128)S(1)}, f32[8,16,8,256]{3,1,2,0:T(8,128)S(1)}, ...), condition=%wide.region_1.2_spmd, body=%wide.region_0.1_spmd.sunk | while | flops 222494848 | bytes 1852517 | solution.py:95
  50.2 25.9 %fusion.48 = f32[1,4,8,128]{3,1,2,0:T(4,128)S(1)} fusion(f32[16,8,256]{2,0,1:T(8,128)S(1)} %get-tuple-element.131, f32[16,8,256]{2,0,1:T(8,128)S(1)} %get-tuple-element.132, f32[16,8,256]{2,0,1:T(8,128)S(1)} %get-tuple-element.133, f32[16,8,256]{2,0,1:T(8,128)S(1)} %get-tuple-element.134, f32[128]{0:T(128)S(1)} %iota_convert_fusion.2, ...), kind=kOutput, calls=%fused_computation.14.clone.3 | convolution fusion | flops 222429184 | bytes 705024 | tf_op jit(solution)/shard_map/while/body/eval_jaxpr/bkri,krim->brm/dot_general | solution.py:93
  76.3 25.9 %fusion.48 = f32[1,4,8,128]{3,1,2,0:T(4,128)S(1)} fusion(f32[16,8,256]{2,0,1:T(8,128)S(1)} %get-tuple-element.131, f32[16,8,256]{2,0,1:T(8,128)S(1)} %get-tuple-element.132, f32[16,8,256]{2,0,1:T(8,128)S(1)} %get-tuple-element.133, f32[16,8,256]{2,0,1:T(8,128)S(1)} %get-tuple-element.134, f32[128]{0:T(128)S(1)} %iota_convert_fusion.2, ...), kind=kOutput, calls=%fused_computation.14.clone.3 | convolution fusion | flops 222429184 | bytes 705024 | tf_op jit(solution)/shard_map/while/body/eval_jaxpr/bkri,krim->brm/dot_general | solution.py:93
  102.3 25.9 %fusion.48 = f32[1,4,8,128]{3,1,2,0:T(4,128)S(1)} fusion(f32[16,8,256]{2,0,1:T(8,128)S(1)} %get-tuple-element.131, f32[16,8,256]{2,0,1:T(8,128)S(1)} %get-tuple-element.132, f32[16,8,256]{2,0,1:T(8,128)S(1)} %get-tuple-element.133, f32[16,8,256]{2,0,1:T(8,128)S(1)} %get-tuple-element.134, f32[128]{0:T(128)S(1)} %iota_convert_fusion.2, ...), kind=kOutput, calls=%fused_computation.14.clone.3 | convolution fusion | flops 222429184 | bytes 705024 | tf_op jit(solution)/shard_map/while/body/eval_jaxpr/bkri,krim->brm/dot_general | solution.py:93
  128.4 25.9 %fusion.48 = f32[1,4,8,128]{3,1,2,0:T(4,128)S(1)} fusion(f32[16,8,256]{2,0,1:T(8,128)S(1)} %get-tuple-element.131, f32[16,8,256]{2,0,1:T(8,128)S(1)} %get-tuple-element.132, f32[16,8,256]{2,0,1:T(8,128)S(1)} %get-tuple-element.133, f32[16,8,256]{2,0,1:T(8,128)S(1)} %get-tuple-element.134, f32[128]{0:T(128)S(1)} %iota_convert_fusion.2, ...), kind=kOutput, calls=%fused_computation.14.clone.3 | convolution fusion | flops 222429184 | bytes 705024 | tf_op jit(solution)/shard_map/while/body/eval_jaxpr/bkri,krim->brm/dot_general | solution.py:93
  154.4 25.9 %fusion.48 = f32[1,4,8,128]{3,1,2,0:T(4,128)S(1)} fusion(f32[16,8,256]{2,0,1:T(8,128)S(1)} %get-tuple-element.131, f32[16,8,256]{2,0,1:T(8,128)S(1)} %get-tuple-element.132, f32[16,8,256]{2,0,1:T(8,128)S(1)} %get-tuple-element.133, f32[16,8,256]{2,0,1:T(8,128)S(1)} %get-tuple-element.134, f32[128]{0:T(128)S(1)} %iota_convert_fusion.2, ...), kind=kOutput, calls=%fused_computation.14.clone.3 | convolution fusion | flops 222429184 | bytes 705024 | tf_op jit(solution)/shard_map/while/body/eval_jaxpr/bkri,krim->brm/dot_general | solution.py:93
  180.5 25.9 %fusion.48 = f32[1,4,8,128]{3,1,2,0:T(4,128)S(1)} fusion(f32[16,8,256]{2,0,1:T(8,128)S(1)} %get-tuple-element.131, f32[16,8,256]{2,0,1:T(8,128)S(1)} %get-tuple-element.132, f32[16,8,256]{2,0,1:T(8,128)S(1)} %get-tuple-element.133, f32[16,8,256]{2,0,1:T(8,128)S(1)} %get-tuple-element.134, f32[128]{0:T(128)S(1)} %iota_convert_fusion.2, ...), kind=kOutput, calls=%fused_computation.14.clone.3 | convolution fusion | flops 222429184 | bytes 705024 | tf_op jit(solution)/shard_map/while/body/eval_jaxpr/bkri,krim->brm/dot_general | solution.py:93
  206.5 25.9 %fusion.48 = f32[1,4,8,128]{3,1,2,0:T(4,128)S(1)} fusion(f32[16,8,256]{2,0,1:T(8,128)S(1)} %get-tuple-element.131, f32[16,8,256]{2,0,1:T(8,128)S(1)} %get-tuple-element.132, f32[16,8,256]{2,0,1:T(8,128)S(1)} %get-tuple-element.133, f32[16,8,256]{2,0,1:T(8,128)S(1)} %get-tuple-element.134, f32[128]{0:T(128)S(1)} %iota_convert_fusion.2, ...), kind=kOutput, calls=%fused_computation.14.clone.3 | convolution fusion | flops 222429184 | bytes 705024 | tf_op jit(solution)/shard_map/while/body/eval_jaxpr/bkri,krim->brm/dot_general | solution.py:93
  232.6 25.9 %fusion.48 = f32[1,4,8,128]{3,1,2,0:T(4,128)S(1)} fusion(f32[16,8,256]{2,0,1:T(8,128)S(1)} %get-tuple-element.131, f32[16,8,256]{2,0,1:T(8,128)S(1)} %get-tuple-element.132, f32[16,8,256]{2,0,1:T(8,128)S(1)} %get-tuple-element.133, f32[16,8,256]{2,0,1:T(8,128)S(1)} %get-tuple-element.134, f32[128]{0:T(128)S(1)} %iota_convert_fusion.2, ...), kind=kOutput, calls=%fused_computation.14.clone.3 | convolution fusion | flops 222429184 | bytes 705024 | tf_op jit(solution)/shard_map/while/body/eval_jaxpr/bkri,krim->brm/dot_general | solution.py:93
  258.5 0.8 concatenate.11
  259.3 2.7 broadcast_in_dim.93
  262.0 3.7 %all-to-all-start.2 = ((f32[16,1,37504]{2,1,0:T(1,128)}), f32[16,1,37504]{2,1,0:T(1,128)S(1)}, u32[]{:S(2)}, u32[]{:S(2)}) async-start(f32[16,1,37504]{2,1,0:T(1,128)} %broadcast_in_dim.93), calls=%async_computation.2 | async-start | bytes 4800512 | tf_op jit(solution)/shard_map/all_to_all | solution.py:18
  265.7 33.2 %all-to-all-done.2 = f32[16,1,37504]{2,1,0:T(1,128)S(1)} async-done(((f32[16,1,37504]{2,1,0:T(1,128)}), f32[16,1,37504]{2,1,0:T(1,128)S(1)}, u32[]{:S(2)}, u32[]{:S(2)}) %all-to-all-start.2) | async-done | bytes 2400288 | tf_op jit(solution)/shard_map/all_to_all | solution.py:18
  298.9 1.5 reduce_sum.57
  300.5 0.7 slice_multiply_fusion
  301.4 0.7 reduce_window_sum.22
  302.5 0.6 broadcast_in_dim.95
  303.1 8.6 %all-to-all-start.3 = ((f32[16,1,4]{2,1,0:T(1,128)}), f32[16,1,4]{2,1,0:T(1,128)S(1)}, u32[]{:S(2)}, u32[]{:S(2)}) async-start(f32[16,1,4]{2,1,0:T(1,128)} %broadcast_in_dim.95), calls=%async_computation.3 | async-start | bytes 16384 | tf_op jit(solution)/shard_map/all_to_all | solution.py:18
  311.7 0.6 subtract_multiply_fusion
  312.5 0.7 copy.68
  313.2 4.7 %all-to-all-done.3 = f32[16,1,4]{2,1,0:T(1,128)S(1)} async-done(((f32[16,1,4]{2,1,0:T(1,128)}), f32[16,1,4]{2,1,0:T(1,128)S(1)}, u32[]{:S(2)}, u32[]{:S(2)}) %all-to-all-start.3) | async-done | bytes 288 | tf_op jit(solution)/shard_map/all_to_all | solution.py:18
  318.8 0.7 add_multiply_fusion
  (91 shorter events, 3.7 us)
Async XLA Ops:
  1.4 29.2 %collective-permute-start.1 = (f32[256]{0:T(256)S(1)}, f32[256]{0:T(256)S(1)}, u32[]{:S(2)}, u32[]{:S(2)}) collective-permute-start(f32[256]{0:T(256)S(1)} %bitcast.84), channel_id=1, source_target_pairs={{1,0},{2,1},{3,2},{4,3},{5,4},{6,5},{7,6},{8,7},{9,8},{10,9},{11,1... | collective-permute-start | bytes 3080 | tf_op jit(solution)/shard_map/ppermute | solution.py:44
  3.9 16.8 %all-to-all-start.1 = ((f32[16,1,256]{2,1,0:T(1,128)}), f32[16,1,256]{2,1,0:T(1,128)S(1)}, u32[]{:S(2)}, u32[]{:S(2)}) async-start(f32[16,1,256]{2,1,0:T(1,128)} %broadcast_in_dim.90), calls=%async_computation.1 | async-start | bytes 32768 | tf_op jit(solution)/shard_map/all_to_all | solution.py:18
  12.0 30.2 %collective-permute-start = (f32[16,256]{0,1:T(8,128)S(1)}, f32[16,256]{0,1:T(8,128)S(1)}, u32[]{:S(2)}, u32[]{:S(2)}) collective-permute-start(f32[16,256]{0,1:T(8,128)S(1)} %bitcast.76), channel_id=1, source_target_pairs={{1,0},{2,1},{3,2},{4,3},{5,4},{6,5},{7,6},{8,7},{9,8},{10,9},{11,1... | collective-permute-start | bytes 49160 | tf_op jit(solution)/shard_map/ppermute | solution.py:44
  15.5 15.0 %copy-start.5 = (s32[256]{0:T(256)S(1)}, s32[256]{0:T(256)}, u32[]{:S(2)}) copy-start(s32[256]{0:T(256)} %param.19) | copy-start | bytes 3076
  15.5 15.0 %copy-start.1 = (s32[64,256]{1,0:T(8,128)S(1)}, s32[64,256]{1,0:T(8,128)}, u32[]{:S(2)}) copy-start(s32[64,256]{1,0:T(8,128)} %param.17) | copy-start | bytes 196612
  21.4 21.0 %copy-start = (f32[16,64,256]{2,1,0:T(8,128)S(1)}, f32[16,64,256]{2,1,0:T(8,128)}, u32[]{:S(2)}) copy-start(f32[16,64,256]{2,1,0:T(8,128)} %param.12) | copy-start | bytes 3145732
  21.4 21.0 %copy-start.4 = (f32[64,256]{1,0:T(8,128)S(1)}, f32[64,256]{1,0:T(8,128)}, u32[]{:S(2)}) copy-start(f32[64,256]{1,0:T(8,128)} %param.14) | copy-start | bytes 196612
  21.4 16.5 %all-to-all-start = ((f32[16,16,256]{2,1,0:T(8,128)}), f32[16,16,256]{2,1,0:T(8,128)S(1)}, u32[]{:S(2)}, u32[]{:S(2)}) async-start(f32[16,16,256]{2,1,0:T(8,128)} %broadcast_in_dim.86), calls=%async_computation | async-start | bytes 524288 | tf_op jit(solution)/shard_map/all_to_all | solution.py:18
  42.4 2.4 copy-start.2
  48.8 1.2 copy-start.3
  262.0 37.0 %all-to-all-start.2 = ((f32[16,1,37504]{2,1,0:T(1,128)}), f32[16,1,37504]{2,1,0:T(1,128)S(1)}, u32[]{:S(2)}, u32[]{:S(2)}) async-start(f32[16,1,37504]{2,1,0:T(1,128)} %broadcast_in_dim.93), calls=%async_computation.2 | async-start | bytes 4800512 | tf_op jit(solution)/shard_map/all_to_all | solution.py:18
  303.1 14.8 %all-to-all-start.3 = ((f32[16,1,4]{2,1,0:T(1,128)}), f32[16,1,4]{2,1,0:T(1,128)S(1)}, u32[]{:S(2)}, u32[]{:S(2)}) async-start(f32[16,1,4]{2,1,0:T(1,128)} %broadcast_in_dim.95), calls=%async_computation.3 | async-start | bytes 16384 | tf_op jit(solution)/shard_map/all_to_all | solution.py:18
where the time goes:
time: 322 us; the launch traced here: 319 us
  matrix products  210 us (65%)
  waiting for transfers between devices  45.3 us (14%)
  starting transfers between devices  30.5 us (9%)
  local copies, waits for them, and re-layouts  20.7 us (6%)
  other arithmetic  11.5 us (4%)
    dot_general x8, matrix products, one_block(): jnp.einsum('bkri,krim->brm', weighted, tent, precision=lax.Precision.HIGH...  207 us
    all_to_all x4, waiting for transfers between devices, copy_for_each(): return lax.all_to_all(copies, axis, split_axis=0, concat_axis=0, tiled=True)  45.3 us
    all_to_all x4, starting transfers between devices, copy_for_each(): return lax.all_to_all(copies, axis, split_axis=0, concat_axis=0, tiled=True)  26.7 us
  transfers between devices with their start and end apart: 6, of which 3 were waited for; matrix products, arithmetic and copies ran while one was open for 5% of the time, Pallas kernels for 0%

commit v1 on v0

v1 whole, which is shorter than its diff:
```python
import functools
import math

import jax
import jax.numpy as jnp
from jax import lax
from jax.experimental import pallas as pl
from jax.experimental.pallas import tpu as pltpu
from jax.sharding import PartitionSpec as P

THERMAL_BINS = 128
OCEAN_REGIONS = 4
THERMAL_FLOOR = -2.0
THERMAL_RANGE = 32.0

ROWS = 8
LOW = 8
HIGH = THERMAL_BINS // LOW
GROUPS = OCEAN_REGIONS * HIGH
LANES = 128
EDGE = 24
PARCEL = 24
HEAT, FLUX, SOUTH, MEAN, WET = 64, 68, 72, 76, 77


def split_in_two(x):
    high = x.astype(jnp.bfloat16).astype(jnp.float32)
    return high, x - high


def bin_rows(
    theta, speed, tier, zonal, plan, energy, depth, label, next_row, next_depth, parts, parcel
):
    levels = theta.shape[0]
    width = theta.shape[2]
    row_id = lax.broadcasted_iota(jnp.int32, (ROWS, width), 0)
    last_row = row_id == ROWS - 1

    def northern(own, beyond):
        return jnp.where(last_row, beyond, pltpu.roll(own, ROWS - 1, 0))

    own_depth = depth[...].astype(jnp.float32)
    face_depth = jnp.minimum(own_depth, northern(own_depth, next_depth()))
    basin = label[...]
    basin_base = basin.astype(jnp.float32) * float(HIGH)
    in_basin = [basin == b for b in range(OCEAN_REGIONS)]
    span = zonal[...]
    lane = lax.broadcasted_iota(jnp.int32, (ROWS, LANES), 1)
    terms = jnp.zeros((ROWS, LANES), jnp.float32)

    def over_longitude(x):
        return jnp.sum(x, axis=1, keepdims=True)

    running = [jnp.zeros((ROWS, 1), jnp.float32) for _ in range(OCEAN_REGIONS)]
    mean_sum = jnp.zeros((ROWS, width), jnp.float32)
    wet_sum = jnp.zeros((ROWS, width), jnp.float32)
    heat_sum = jnp.zeros((ROWS, width), jnp.float32)
    per_bin = THERMAL_BINS / THERMAL_RANGE
    for k in range(levels):
        own = theta[k]
        face = 0.5 * (own + northern(own, next_row(k)))
        volume = jnp.where(face_depth > float(k), tier[k] * span, 0.0)
        transport = volume * speed[k]
        position = jnp.clip((face - THERMAL_FLOOR) * per_bin, 0.0, THERMAL_BINS - 1.0)
        low_bin = jnp.minimum(jnp.floor(position), THERMAL_BINS - 2.0)
        high_weight = position - low_bin
        digit = jnp.floor(low_bin * (1.0 / LOW))
        weighted = transport * high_weight
        parts[0, k] = basin_base + digit
        parts[1, k] = low_bin - LOW * digit
        parts[2, k], parts[3, k] = split_in_two(transport)
        parts[4, k], parts[5, k] = split_in_two(weighted)
        mean_sum += volume * face
        wet_sum += volume
        heat_sum += transport * face
        for b in range(OCEAN_REGIONS):
            running[b] += over_longitude(jnp.where(in_basin[b], transport, 0.0))
            terms = jnp.where(lane == b * levels + k, running[b], terms)
    flux = energy[...] * plan[...]
    for b in range(OCEAN_REGIONS):
        terms = jnp.where(
            lane == HEAT + b, over_longitude(jnp.where(in_basin[b], heat_sum, 0.0)), terms
        )
        terms = jnp.where(
            lane == FLUX + b, over_longitude(jnp.where(in_basin[b], flux, 0.0)), terms
        )
    terms = jnp.where(lane == MEAN, over_longitude(mean_sum), terms)
    terms = jnp.where(lane == WET, over_longitude(wet_sum), terms)

    packed_id = lax.broadcasted_iota(jnp.int32, (16, width), 0)
    group_ids = [
        (packed_id + 16 * t).astype(jnp.float32).astype(jnp.bfloat16) for t in range(GROUPS // 16)
    ]
    low_ids = (packed_id & (LOW - 1)).astype(jnp.float32).astype(jnp.bfloat16)
    one = jnp.ones((16, width), jnp.bfloat16)
    none = jnp.zeros((16, width), jnp.bfloat16)

    def spread(q, k, r, count):
        return jnp.broadcast_to(parts[q, k, r : r + 1, :], (count, width))

    sums = []
    for r in range(ROWS):
        values, groups = [], []
        for k in range(levels):
            group = spread(0, k, r, 16).astype(jnp.bfloat16)
            groups.append(
                jnp.concatenate([jnp.where(group == g, one, none) for g in group_ids], axis=0)
            )
            at_low = spread(1, k, r, 16).astype(jnp.bfloat16) == low_ids
            pair = [
                jnp.concatenate([spread(q, k, r, 8), spread(q + 1, k, r, 8)], axis=0).astype(
                    jnp.bfloat16
                )
                for q in (2, 4)
            ]
            values.append(
                jnp.concatenate([jnp.where(at_low, v, none) for v in pair], axis=0)
            )
        sums.append(
            lax.dot_general(
                jnp.concatenate(values, axis=1),
                jnp.concatenate(groups, axis=1),
                (((1,), (1,)), ((), ())),
                preferred_element_type=jnp.float32,
            )
        )

    low_id = lax.broadcasted_iota(jnp.int32, (LOW, LANES), 0)
    classes = []
    for r in range(0, ROWS, 2):
        both = jnp.concatenate([sums[r], sums[r + 1]], axis=1)
        plain = both[0:8] + both[8:16]
        upper = both[16:24] + both[24:32]
        moved = pltpu.roll(upper, 1, 0)
        moved = jnp.where(low_id == 0, pltpu.roll(moved, 1, 1), moved)
        classes.append(plain - upper + moved)

    place_id = lax.broadcasted_iota(jnp.int32, (16, LANES), 0)
    lane16 = lax.broadcasted_iota(jnp.int32, (16, LANES), 1)
    of_place = (place_id & 1) * OCEAN_REGIONS + (place_id >> 2) == (lane16 >> 4)
    first = of_place & ((place_id & 2) == 0)
    second = of_place & ((place_id & 2) != 0)
    zero = jnp.zeros((16, LANES), jnp.float32)
    from_id = lax.broadcasted_iota(jnp.int32, (LANES, LANES), 0)
    to_id = lax.broadcasted_iota(jnp.int32, (LANES, LANES), 1)
    target = (from_id & (HIGH - 1)) * LOW
    placing = jnp.concatenate(
        [jnp.where(to_id == target + low, 1.0, 0.0) for low in range(LOW)], axis=0
    ).astype(jnp.bfloat16)
    rows = []
    for d in range(2):
        rows.append(
            jnp.concatenate(
                [
                    jnp.where(
                        first,
                        jnp.broadcast_to(classes[2 * d][low : low + 1], (16, LANES)),
                        jnp.where(
                            second,
                            jnp.broadcast_to(classes[2 * d + 1][low : low + 1], (16, LANES)),
                            zero,
                        ),
                    )
                    for low in range(LOW)
                ],
                axis=1,
            )
        )
    wide = jnp.concatenate(rows, axis=0)
    wide_high, wide_low = split_in_two(wide)
    placed = jnp.dot(
        jnp.concatenate([wide_high, wide_low], axis=0).astype(jnp.bfloat16),
        placing,
        preferred_element_type=jnp.float32,
    )
    placed = placed[0:32] + placed[32:64]
    for d in range(2):
        parcel[d, 0:16, :] = placed[16 * d : 16 * d + 16]
    return terms


def store_terms(parcel, terms):
    parcel[0, 16:24, :] = terms
    parcel[1, 16:24, :] = pltpu.roll(terms, 4, 0)


def early_kernel(
    theta, beyond, speed, tier, zonal, plan, energy, depth, depth_beyond, label, parcel, parts
):
    terms = bin_rows(
        theta,
        speed,
        tier,
        zonal,
        plan,
        energy,
        depth,
        label,
        lambda k: jnp.broadcast_to(beyond[k, 0:1, :], theta.shape[1:]),
        lambda: jnp.broadcast_to(depth_beyond[0:1, :], theta.shape[1:]).astype(jnp.float32),
        parts,
        parcel,
    )
    store_terms(parcel, terms)


def late_kernel(
    where_to,
    theta,
    speed,
    tier,
    zonal,
    plan,
    energy,
    depth,
    label,
    halo,
    fold_a,
    fold_b,
    south,
    so_far,
    parcel,
    parts,
    edge,
):
    del so_far
    shape = theta.shape[1:]
    width = shape[1]
    columns = jnp.concatenate([fold_a[0], fold_b[0]], axis=1)
    high, rest = split_in_two(columns)
    middle, lowest = split_in_two(rest)
    source = lax.broadcasted_iota(jnp.int32, (2 * width, width), 0)
    target = lax.broadcasted_iota(jnp.int32, (2 * width, width), 1)
    mirror = jnp.where(source + target == where_to[2] + (width - 1), 1.0, 0.0).astype(jnp.bfloat16)
    pieces = jnp.dot(
        jnp.concatenate([high, middle, lowest], axis=0).astype(jnp.bfloat16),
        mirror,
        preferred_element_type=jnp.float32,
    )
    folded = pieces[0:EDGE] + pieces[EDGE : 2 * EDGE] + pieces[2 * EDGE : 3 * EDGE]
    edge[...] = jnp.where(where_to[3] == 1, folded, halo[...])
    levels = theta.shape[0]
    terms = bin_rows(
        theta,
        speed,
        tier,
        zonal,
        plan,
        energy,
        depth,
        label,
        lambda k: jnp.broadcast_to(edge[k : k + 1, :], shape),
        lambda: jnp.broadcast_to(edge[levels : levels + 1, :], shape),
        parts,
        parcel,
    )
    further = lax.broadcasted_iota(jnp.int32, south.shape, 0) < where_to[4]
    offset = jnp.sum(jnp.where(further, south[...], 0.0), axis=0, keepdims=True)
    last = lax.broadcasted_iota(jnp.int32, terms.shape, 0) == ROWS - 1
    terms = terms + jnp.where(last, jnp.broadcast_to(offset, terms.shape), 0.0)
    store_terms(parcel, terms)


def finish_kernel(unit_scale, implied_scale, parcels, class_out, stream, heat, implied):
    devices = parcels.shape[0]
    rows = 4 * devices
    levels = stream.shape[2]
    for b in range(OCEAN_REGIONS):
        for d in range(devices):
            class_out[b, 4 * d : 4 * d + 4, :] = unit_scale * parcels[d, 4 * b : 4 * b + 4, :]
    terms = jnp.concatenate([parcels[d, 16:20, :] for d in range(devices)], axis=0)
    for b in range(OCEAN_REGIONS):
        stream[b] = unit_scale * terms[:, b * levels : (b + 1) * levels]
    turned = jnp.transpose(
        jnp.concatenate([terms, jnp.zeros((LANES - rows, LANES), jnp.float32)], axis=0)
    )
    row_mean = turned[MEAN : MEAN + 1] / jnp.where(
        lax.broadcasted_iota(jnp.int32, (1, LANES), 1) < rows, turned[WET : WET + 1], 1.0
    )
    lane = lax.broadcasted_iota(jnp.int32, (1, LANES), 1)
    for b in range(OCEAN_REGIONS):
        total = turned[(b + 1) * levels - 1 : (b + 1) * levels]
        out = unit_scale / 16.0 * (turned[HEAT + b : HEAT + b + 1] - total * row_mean)
        heat[b : b + 1, :] = out[:, :rows]
        flux = turned[FLUX + b : FLUX + b + 1]
        offset = jnp.sum(turned[SOUTH + b : SOUTH + b + 1], axis=1, keepdims=True)
        shift = 1
        while shift < rows:
            flux = flux + jnp.where(lane >= shift, pltpu.roll(flux, shift, 1), 0.0)
            shift *= 2
        implied[b : b + 1, :] = (implied_scale * (flux + offset))[:, :rows]


def exchanged(pieces, axis):
    return lax.all_to_all(pieces, axis, split_axis=0, concat_axis=0, tiled=True)


def copies(array, axis):
    return jnp.broadcast_to(array, (lax.axis_size(axis), *array.shape))


def body(
    meridional_speed,
    theta_field,
    tier_vertical_span,
    grid_zonal_span,
    grid_plan_extent,
    ocean_energy_input,
    ocean_tier_tally,
    grid_region_label,
    seam_matching_meridian,
):
    levels, parallels, width = theta_field.shape
    lon_size = lax.axis_size("lon")
    lat_size = lax.axis_size("lat")
    lat_index = lax.axis_index("lat")
    width_total = width * lon_size
    unit_scale = math.sqrt(THERMAL_BINS / (width_total * levels))
    implied_scale = 2.0 / math.sqrt(width_total * parallels * lat_size)
    blocks = parallels // ROWS

    def edge_of(row):
        depth = ocean_tier_tally[row][None].astype(jnp.float32)
        return jnp.concatenate(
            [theta_field[:, row, :], depth, jnp.zeros((EDGE - levels - 1, width), jnp.float32)]
        )

    halo = lax.ppermute(edge_of(0), "lat", [(i + 1, i) for i in range(lat_size - 1)])
    fold = exchanged(copies(edge_of(parallels - 1), "lon"), "lon")
    flux = ocean_energy_input * grid_plan_extent
    flux_totals = jnp.stack(
        [jnp.sum(jnp.where(grid_region_label == b, flux, 0.0)) for b in range(OCEAN_REGIONS)]
    )
    flux_lanes = jnp.pad(flux_totals, (SOUTH, LANES - SOUTH - OCEAN_REGIONS))
    south = exchanged(copies(flux_lanes, "lat"), "lat")

    start = (seam_matching_meridian[0] + (width_total - (width - 1))) % width_total
    first = start // width
    where_to = jnp.stack(
        [
            first,
            (first + 1) % lon_size,
            start % width,
            (lat_index == lat_size - 1).astype(jnp.int32),
            lat_index.astype(jnp.int32),
        ]
    )

    def field(index):
        return pl.BlockSpec((levels, ROWS, width), lambda i, *s: (0, index(i), 0))

    def plane(index):
        return pl.BlockSpec((ROWS, width), lambda i, *s: (index(i), 0))

    parcel_shape = jax.ShapeDtypeStruct((2 * blocks, PARCEL, LANES), jnp.float32)
    parts_shape = pltpu.VMEM((6, levels, ROWS, width), jnp.float32)
    in_smem = pl.BlockSpec(memory_space=pltpu.SMEM)
    here, after = (lambda i: i), (lambda i: i + 1)
    parcels = pl.pallas_call(
        early_kernel,
        grid=(blocks - 1,),
        in_specs=[
            field(here),
            field(after),
            field(here),
            in_smem,
            plane(here),
            plane(here),
            plane(here),
            plane(here),
            plane(after),
            plane(here),
        ],
        out_specs=pl.BlockSpec((2, PARCEL, LANES), lambda i: (i, 0, 0)),
        out_shape=parcel_shape,
        scratch_shapes=[parts_shape],
        cost_estimate=pl.CostEstimate(
            flops=8_000_000_000, bytes_accessed=4_000_000, transcendentals=0
        ),
        name="early_rows",
    )(
        theta_field,
        theta_field,
        meridional_speed,
        tier_vertical_span,
        grid_zonal_span,
        grid_plan_extent,
        ocean_energy_input,
        ocean_tier_tally,
        ocean_tier_tally,
        grid_region_label,
    )
    final = lambda i: blocks - 1
    whole = lambda *shape: pl.BlockSpec(shape, lambda i, s: (0,) * len(shape))
    parcels = pl.pallas_call(
        late_kernel,
        grid_spec=pltpu.PrefetchScalarGridSpec(
            num_scalar_prefetch=1,
            grid=(1,),
            in_specs=[
                field(final),
                field(final),
                in_smem,
                plane(final),
                plane(final),
                plane(final),
                plane(final),
                plane(final),
                whole(EDGE, width),
                pl.BlockSpec((1, EDGE, width), lambda i, s: (s[0], 0, 0)),
                pl.BlockSpec((1, EDGE, width), lambda i, s: (s[1], 0, 0)),
                whole(lat_size, LANES),
                pl.BlockSpec(memory_space=pl.ANY),
            ],
            out_specs=pl.BlockSpec((2, PARCEL, LANES), lambda i, s: (blocks - 1, 0, 0)),
            scratch_shapes=[parts_shape, pltpu.VMEM((EDGE, width), jnp.float32)],
        ),
        out_shape=parcel_shape,
        input_output_aliases={13: 0},
        cost_estimate=pl.CostEstimate(
            flops=1_000_000_000, bytes_accessed=600_000, transcendentals=0
        ),
        name="late_rows",
    )(
        where_to,
        theta_field,
        meridional_speed,
        tier_vertical_span,
        grid_zonal_span,
        grid_plan_extent,
        ocean_energy_input,
        ocean_tier_tally,
        grid_region_label,
        halo,
        fold,
        fold,
        south,
        parcels,
    )
    own = jnp.sum(exchanged(parcels, "lon"), axis=0)
    everyone = exchanged(copies(own, "lon"), "lon")
    return pl.pallas_call(
        functools.partial(finish_kernel, unit_scale, implied_scale),
        out_shape=(
            jax.ShapeDtypeStruct((OCEAN_REGIONS, parallels, THERMAL_BINS), jnp.float32),
            jax.ShapeDtypeStruct((OCEAN_REGIONS, parallels, levels), jnp.float32),
            jax.ShapeDtypeStruct((OCEAN_REGIONS, parallels), jnp.float32),
            jax.ShapeDtypeStruct((OCEAN_REGIONS, parallels), jnp.float32),
        ),
        name="finish_rows",
    )(everyone)


def solution(mesh):
    in_specs = (
        P(None, "lat", "lon"),
        P(None, "lat", "lon"),
        P(),
        P("lat", "lon"),
        P("lat", "lon"),
        P("lat", "lon"),
        P("lat", "lon"),
        P("lat", "lon"),
        P("lon"),
    )
    out_specs = (P(None, "lat", None), P(None, "lat", None), P(None, "lat"), P(None, "lat"))
    return jax.shard_map(body, mesh=mesh, in_specs=in_specs, out_specs=out_specs, check_vma=False)
```

time: 322 us -> 79.6 us (0.25)
  matrix products: 210 us -> 0 us
  waiting for transfers between devices: 45.3 us -> 2.25 us
  blocking collectives: 0 us -> 27 us
  Pallas kernels: 0 us -> 19.4 us
  local copies, waits for them, and re-layouts: 20.7 us -> 5.98 us
  starting transfers between devices: 30.5 us -> 17.6 us
  other arithmetic: 11.5 us -> 5.03 us
    dot_general x11 -> x0, matrix products: 210 us -> none  [the longest x8 207 us: one_block(): jnp.einsum('bkri,krim->brm', weighted, tent, precision=lax.Precision.HIGH...]
    all_to_all x4 -> x2, waiting for transfers between devices: 45.3 us -> 2.24 us  [exchanged(): return lax.all_to_all(pieces, axis, split_axis=0, concat_axis=0, tiled=True)]
    all_to_all x0 -> x2, blocking collectives: none -> 27 us  [exchanged(): return lax.all_to_all(pieces, axis, split_axis=0, concat_axis=0, tiled=True)]
    pallas_call x0 -> x3, Pallas kernels: none -> 19.4 us  [the longest x1 13.2 us: body(): pl.pallas_call(early_kernel, grid=(blocks - 1,), in_specs=[field(here), f...]
    all_to_all x4 -> x2, starting transfers between devices: 26.7 us -> 15.6 us  [exchanged(): return lax.all_to_all(pieces, axis, split_axis=0, concat_axis=0, tiled=True)]
    gather x2 -> x0, local copies, waits for them, and re-layouts: 4.03 us -> none  [the longest x1 2.31 us: body(): reflected_theta = jnp.take(seam_theta, seam_matching_meridian, axis=1)]
    broadcast_in_dim x5 -> x3, local copies, waits for them, and re-layouts: 4.67 us -> 1.38 us  [copies(): return jnp.broadcast_to(array, (lax.axis_size(axis), *array.shape))]
  transfers between devices with their start and end apart: 6 -> 3, of which waited for: 3 -> 1; matrix products, arithmetic and copies ran while one was open for 5% -> 5% of each run, Pallas kernels for 0% -> 17%
where the time goes in v1:
time: 79.6 us; the launch traced here: 78.7 us
  blocking collectives  27 us (34%)
  Pallas kernels  19.4 us (24%)
  starting transfers between devices  17.6 us (22%)
  local copies, waits for them, and re-layouts  5.98 us (8%)
  other arithmetic  5.03 us (6%)
  waiting for transfers between devices  2.25 us (3%)
  between operations  1.42 us (2%)
    all_to_all x2, blocking collectives, exchanged(): return lax.all_to_all(pieces, axis, split_axis=0, concat_axis=0, tiled=True)  27 us
    all_to_all x2, starting transfers between devices, exchanged(): return lax.all_to_all(pieces, axis, split_axis=0, concat_axis=0, tiled=True)  15.6 us
    pallas_call x1, Pallas kernels, body(): pl.pallas_call(early_kernel, grid=(blocks - 1,), in_specs=[field(here), f...  13.2 us
    pallas_call x1, Pallas kernels, body(): pl.pallas_call(late_kernel, grid_spec=pltpu.PrefetchScalarGridSpec(num_sc...  4.16 us
    another operation x1, other arithmetic, body(): jnp.stack([jnp.sum(jnp.where(grid_region_label == b, flux, 0.0)) for b in...  2.66 us
    all_to_all x2, waiting for transfers between devices, exchanged(): return lax.all_to_all(pieces, axis, split_axis=0, concat_axis=0, tiled=True)  2.24 us
    pallas_call x1, Pallas kernels, body(): pl.pallas_call(functools.partial(finish_kernel, unit_scale, implied_scale...  2.08 us
    ppermute x1, starting transfers between devices, body(): lax.ppermute(edge_of(0), 'lat', [(i + 1, i) for i in range(lat_size - 1)])  2.01 us
  transfers between devices with their start and end apart: 3, of which 1 were waited for; matrix products, arithmetic and copies ran while one was open for 5% of the time, Pallas kernels for 17%

profile of v1, /device:TPU:32, one launch (start us, length us, event | category | flops | bytes accessed | tf_op | source)
XLA Modules:
  0.0 78.7 jit_solution(7157393396518830353)
XLA Ops:
  0.6 1.5 %select_reduce_fusion.3 = (f32[]{:T(128)}, f32[]{:T(128)}, f32[]{:T(128)}, f32[]{:T(128)}) fusion(s32[64,256]{1,0:T(8,128)} %label.3, f32[64,256]{1,0:T(8,128)} %energy.3, f32[64,256]{1,0:T(8,128)} %plan.3), kind=kLoop, calls=%fused_computation.3 | loop fusion | flops 212988 | bytes 196624 | tf_op jit(solution)/shard_map/reduce_sum | solution.py:332
  2.2 2.7 %select_maximum_fusion = f32[128]{0:T(128)S(1)} fusion(f32[1]{0:T(128)} %bitcast.11, f32[1]{0:T(128)} %bitcast.10, f32[1]{0:T(128)} %bitcast.9, f32[1]{0:T(128)} %bitcast.8), kind=kLoop, calls=%fused_computation.11 | loop fusion | flops 1280 | bytes 528 | tf_op jit(solution)/shard_map/stack | solution.py:331
  4.8 0.6 broadcast_in_dim.18
  5.4 8.6 %all-to-all-start.1 = ((f32[16,1,128]{2,1,0:T(1,128)}), f32[16,1,128]{2,1,0:T(1,128)S(1)}, u32[]{:S(2)}, u32[]{:S(2)}) async-start(f32[16,1,128]{2,1,0:T(1,128)} %broadcast_in_dim.18), calls=%async_computation.1 | async-start | bytes 16384 | tf_op jit(solution)/shard_map/all_to_all | solution.py:295
  14.0 0.7 slice_convert_fusion
  14.8 1.0 %fusion = (f32[16,1,256]{2,1,0:T(1,128)S(1)}, f32[16,1,256]{2,1,0:T(1,128)S(1)}) fusion(f32[16,64,256]{2,1,0:T(8,128)} %theta.3), kind=kLoop, calls=%fused_computation.14 | loop fusion | bytes 65536 | tf_op jit(solution)/shard_map/slice | solution.py:325
  15.8 0.1 pad.14.clone
  15.8 0.1 maximum_maximum_fusion.1
  15.9 2.0 %collective-permute-start = (f32[24,256]{1,0:T(8,128)S(1)}, f32[24,256]{1,0:T(8,128)S(1)}, u32[]{:S(2)}, u32[]{:S(2)}) collective-permute-start(f32[24,256]{1,0:T(8,128)S(1)} %get-tuple-element.25), channel_id=1, source_target_pairs={{1,0},{2,1},{3,2},{4,3},{5,4},{6,5},{7,6},{8,7},{9,8},{10,9},{11,1... | collective-permute-start | bytes 73736 | tf_op jit(solution)/shard_map/ppermute | solution.py:328
  17.9 2.2 %all-to-all-done.1 = f32[16,1,128]{2,1,0:T(1,128)S(1)} async-done(((f32[16,1,128]{2,1,0:T(1,128)}), f32[16,1,128]{2,1,0:T(1,128)S(1)}, u32[]{:S(2)}, u32[]{:S(2)}) %all-to-all-start.1) | async-done | bytes 8224 | tf_op jit(solution)/shard_map/all_to_all | solution.py:295
  20.2 0.0 copy-start.1
  20.2 0.8 broadcast_in_dim.16
  20.9 0.0 copy-done.1
  21.0 7.0 %all-to-all-start = ((f32[16,24,256]{2,1,0:T(8,128)}), f32[16,24,256]{2,1,0:T(8,128)S(1)}, u32[]{:S(2)}, u32[]{:S(2)}) async-start(f32[16,24,256]{2,1,0:T(8,128)} %broadcast_in_dim.16), calls=%async_computation | async-start | bytes 786432 | tf_op jit(solution)/shard_map/all_to_all | solution.py:295
  28.0 0.0 copy-start.3
  28.0 13.2 %early_rows.1.so_far = f32[16,24,128]{2,1,0:T(8,128)} custom-call(f32[16,64,256]{2,1,0:T(8,128)} %theta.3, f32[16,64,256]{2,1,0:T(8,128)} %theta.3, f32[16,64,256]{2,1,0:T(8,128)} %speed.3, f32[16]{0:T(128)} %tier.3, f32[64,256]{1,0:T(8,128)} %zonal.3, f32[64,256]{1,0:T(8,128)} %plan.3, f32[64,256]{1,0:T(8,128)} %energy.3, s32[64,256]{1,0:T(8,128)} %depth.3, ...), custom_call_target="tpu_custom_call" | custom-call | flops 8000000000 | bytes 4000000 | tf_op jit(solution)/shard_map/early_rows/pallas_call | solution.py:359
  41.2 0.0 copy-done.3
  41.2 0.5 slice.15
  42.4 0.7 stack.42.where_to
  43.1 0.0 collective-permute-done.halo
  43.1 0.0 copy-start.2
  43.1 0.0 all-to-all-done.fold_a.fold_b
  43.1 0.0 copy-start
  43.1 0.6 copy-done.2
  43.7 0.1 copy-done
  43.8 4.2 %late_rows.1 = f32[16,24,128]{2,1,0:T(8,128)} custom-call(s32[5]{0:T(128)} %stack.42.where_to, f32[16,64,256]{2,1,0:T(8,128)} %theta.3, f32[16,64,256]{2,1,0:T(8,128)} %speed.3, f32[16]{0:T(128)} %tier.3, f32[64,256]{1,0:T(8,128)} %zonal.3, f32[64,256]{1,0:T(8,128)} %plan.3, f32[64,256]{1,0:T(8,128)} %energy.3, ...), custom_call_target="tpu_custom_call", output_to_operand_aliasing={{}: (13, {})} | custom-call | flops 1000000000 | bytes 600000 | tf_op jit(solution)/shard_map/late_rows/pallas_call | solution.py:395
  48.0 15.3 %all_to_all.23 = f32[16,24,128]{2,1,0:T(8,128)S(1)} all-to-all(f32[16,24,128]{2,1,0:T(8,128)} %late_rows.1), channel_id=1, replica_groups=mesh['lon'=16,'lat'=16] {'lon'}, dimensions={0} | all-to-all | bytes 393216 | tf_op jit(solution)/shard_map/all_to_all | solution.py:295
  63.3 11.7 %all_to_all.24.parcels = f32[16,24,128]{2,1,0:T(8,128)} all-to-all(f32[16,24,128]{2,1,0:T(8,128)S(1)} %broadcast_in_dim.19), channel_id=1, replica_groups=mesh['lon'=16,'lat'=16] {'lon'}, dimensions={0} | all-to-all | bytes 393216 | tf_op jit(solution)/shard_map/all_to_all | solution.py:295
  75.0 2.1 %finish_rows.1 = (f32[4,64,128]{2,1,0:T(8,128)}, f32[4,64,16]{2,1,0:T(8,128)}, f32[4,64]{1,0:T(4,128)}, f32[4,64]{1,0:T(4,128)}) custom-call(f32[16,24,128]{2,1,0:T(8,128)} %all_to_all.24.parcels), custom_call_target="tpu_custom_call" | custom-call | tf_op jit(solution)/shard_map/finish_rows/pallas_call | solution.py:442
  77.1 1.6 %copy.21 = f32[4,64,16]{1,2,0:T(8,128)} copy(f32[4,64,16]{2,1,0:T(8,128)} %get-tuple-element.13) | data formatting | bytes 32768 | tf_op jit(solution)/shard_map/finish_rows/pallas_call | solution.py:442
  (4 shorter events, 0.0 us)
Async XLA Ops:
  5.4 14.7 %all-to-all-start.1 = ((f32[16,1,128]{2,1,0:T(1,128)}), f32[16,1,128]{2,1,0:T(1,128)S(1)}, u32[]{:S(2)}, u32[]{:S(2)}) async-start(f32[16,1,128]{2,1,0:T(1,128)} %broadcast_in_dim.18), calls=%async_computation.1 | async-start | bytes 16384 | tf_op jit(solution)/shard_map/all_to_all | solution.py:295
  15.9 27.2 %collective-permute-start = (f32[24,256]{1,0:T(8,128)S(1)}, f32[24,256]{1,0:T(8,128)S(1)}, u32[]{:S(2)}, u32[]{:S(2)}) collective-permute-start(f32[24,256]{1,0:T(8,128)S(1)} %get-tuple-element.25), channel_id=1, source_target_pairs={{1,0},{2,1},{3,2},{4,3},{5,4},{6,5},{7,6},{8,7},{9,8},{10,9},{11,1... | collective-permute-start | bytes 73736 | tf_op jit(solution)/shard_map/ppermute | solution.py:328
  20.2 0.8 copy-start.1
  21.0 22.1 %all-to-all-start = ((f32[16,24,256]{2,1,0:T(8,128)}), f32[16,24,256]{2,1,0:T(8,128)S(1)}, u32[]{:S(2)}, u32[]{:S(2)}) async-start(f32[16,24,256]{2,1,0:T(8,128)} %broadcast_in_dim.16), calls=%async_computation | async-start | bytes 786432 | tf_op jit(solution)/shard_map/all_to_all | solution.py:295
  28.0 13.2 %copy-start.3 = (s32[256]{0:T(256)S(1)}, s32[256]{0:T(256)}, u32[]{:S(2)}) copy-start(s32[256]{0:T(256)} %param.17) | copy-start | bytes 3076
  43.1 0.6 copy-start.2
  43.1 0.7 copy-start

commit v2 on v0

v2 whole, which is shorter than its diff:
```python
import functools
import math

import jax
import jax.numpy as jnp
from jax import lax
from jax.experimental import pallas as pl
from jax.experimental.pallas import tpu as pltpu
from jax.sharding import PartitionSpec as P

THERMAL_BINS = 128
OCEAN_REGIONS = 4
THERMAL_FLOOR = -2.0
THERMAL_RANGE = 32.0

ROWS = 8
CHUNK = 16
LOW = 8
HIGH = THERMAL_BINS // LOW
GROUPS = OCEAN_REGIONS * HIGH
LANES = 128
EDGE = 24
TERMS, DEPTHS, TOTALS, EDGES, PARCEL = 16, 20, 22, 24, 56
LAST, LAST_TERMS, SHARE = 20, 24, 32
LAST_THETA, LAST_VOLUME, LAST_SPEED, LAST_DEPTH, LAST_LABEL, LAST_ROWS = 0, 16, 32, 48, 49, 56
HEAT, FLUX, MEAN, WET = 64, 68, 76, 77


def split_in_two(x):
    high = x.astype(jnp.bfloat16).astype(jnp.float32)
    return high, x - high


def over_longitude(x):
    return jnp.sum(x, axis=1, keepdims=True)


def interpolation(face, transport, basin_base):
    per_bin = THERMAL_BINS / THERMAL_RANGE
    position = jnp.clip((face - THERMAL_FLOOR) * per_bin, 0.0, THERMAL_BINS - 1.0)
    low_bin = jnp.minimum(jnp.floor(position), THERMAL_BINS - 2.0)
    digit = jnp.floor(low_bin * (1.0 / LOW))
    weighted = transport * (position - low_bin)
    return (
        basin_base + digit,
        low_bin - LOW * digit,
        *split_in_two(transport),
        *split_in_two(weighted),
    )


class Products:
    def __init__(self, width):
        packed_id = lax.broadcasted_iota(jnp.int32, (16, width), 0)
        as_packed = lambda x: x.astype(jnp.float32).astype(jnp.bfloat16)
        self.group_ids = [as_packed(packed_id + 16 * t) for t in range(GROUPS // 16)]
        self.low_ids = as_packed(packed_id & (LOW - 1))
        self.one = jnp.ones((16, width), jnp.bfloat16)
        self.none = jnp.zeros((16, width), jnp.bfloat16)
        self.width = width

    def row(self, spread, levels):
        values, groups = [], []
        for k in range(levels):
            group = spread(0, k, 16).astype(jnp.bfloat16)
            groups.append(
                jnp.concatenate(
                    [jnp.where(group == g, self.one, self.none) for g in self.group_ids], axis=0
                )
            )
            at_low = spread(1, k, 16).astype(jnp.bfloat16) == self.low_ids
            values.append(
                jnp.concatenate(
                    [
                        jnp.where(
                            at_low,
                            jnp.concatenate([spread(q, k, 8), spread(q + 1, k, 8)], axis=0).astype(
                                jnp.bfloat16
                            ),
                            self.none,
                        )
                        for q in (2, 4)
                    ],
                    axis=0,
                )
            )
        return lax.dot_general(
            jnp.concatenate(values, axis=1),
            jnp.concatenate(groups, axis=1),
            (((1,), (1,)), ((), ())),
            preferred_element_type=jnp.float32,
        )


def class_tile(first, second):
    both = jnp.concatenate([first, second], axis=1)
    plain = both[0:8] + both[8:16]
    upper = both[16:24] + both[24:32]
    moved = pltpu.roll(upper, 1, 0)
    low_id = lax.broadcasted_iota(jnp.int32, (LOW, LANES), 0)
    moved = jnp.where(low_id == 0, pltpu.roll(moved, 1, 1), moved)
    return plain - upper + moved


def rows_kernel(
    theta_hbm,
    speed_hbm,
    tier,
    zonal_hbm,
    plan_hbm,
    energy_hbm,
    depth_hbm,
    label_hbm,
    parcel,
    last,
    theta,
    speed,
    zonal,
    plan,
    energy,
    depth,
    label,
    even,
    odd,
    field_sems,
    plane_sems,
):
    levels, parallels, width = theta.shape
    blocks = parallels // ROWS
    chunks = parallels // CHUNK

    def field_copy(which, c):
        source, target = ((theta_hbm, theta), (speed_hbm, speed))[which]
        rows = pl.ds(c * CHUNK, CHUNK)
        return pltpu.make_async_copy(
            source.at[:, rows, :], target.at[:, rows, :], field_sems.at[which, c]
        )

    planes = [
        pltpu.make_async_copy(s, t, plane_sems.at[n])
        for n, (s, t) in enumerate(
            (
                (depth_hbm, depth),
                (zonal_hbm, zonal),
                (label_hbm, label),
                (energy_hbm, energy),
                (plan_hbm, plan),
            )
        )
    ]
    field_copy(0, 0).start()
    for copy in planes:
        copy.start()
    field_copy(1, 0).start()
    for c in range(1, chunks):
        field_copy(0, c).start()
        field_copy(1, c).start()

    row_id = lax.broadcasted_iota(jnp.int32, (ROWS, width), 0)
    last_row = row_id == ROWS - 1
    lane = lax.broadcasted_iota(jnp.int32, (ROWS, LANES), 1)

    def northern(own, beyond):
        return jnp.where(last_row, jnp.broadcast_to(beyond, own.shape), pltpu.roll(own, ROWS - 1, 0))

    class Block:
        def __init__(self, block, parts):
            self.block, self.parts = block, parts
            self.rows = pl.ds(pl.multiple_of(block * ROWS, ROWS), ROWS)
            ahead = jnp.minimum(block + 1, blocks - 1) * ROWS
            self.beyond = pl.ds(pl.multiple_of(ahead, ROWS), ROWS)
            own_depth = depth[self.rows, :].astype(jnp.float32)
            next_depth = depth[self.beyond, :][0:1].astype(jnp.float32)
            next_depth = jnp.where(block == blocks - 1, 0.0, next_depth)
            self.face_depth = jnp.minimum(own_depth, northern(own_depth, next_depth))
            basin = label[self.rows, :]
            self.basin_base = basin.astype(jnp.float32) * float(HIGH)
            self.in_basin = [basin == b for b in range(OCEAN_REGIONS)]
            self.span = zonal[self.rows, :]
            self.flux = energy[self.rows, :] * plan[self.rows, :]
            self.terms = jnp.zeros((ROWS, LANES), jnp.float32)
            self.running = [jnp.zeros((ROWS, 1), jnp.float32) for _ in range(OCEAN_REGIONS)]
            self.mean_sum = jnp.zeros((ROWS, width), jnp.float32)
            self.wet_sum = jnp.zeros((ROWS, width), jnp.float32)
            self.heat_sum = jnp.zeros((ROWS, width), jnp.float32)

        def level(self, k):
            own = theta[k, self.rows, :]
            face = 0.5 * (own + northern(own, theta[k, self.beyond, :][0:1]))
            volume = jnp.where(self.face_depth > float(k), tier[k] * self.span, 0.0)
            transport = volume * speed[k, self.rows, :]
            for q, value in enumerate(interpolation(face, transport, self.basin_base)):
                self.parts[q, k] = value
            self.mean_sum += volume * face
            self.wet_sum += volume
            self.heat_sum += transport * face
            for b in range(OCEAN_REGIONS):
                self.running[b] += over_longitude(jnp.where(self.in_basin[b], transport, 0.0))
                self.terms = jnp.where(lane == b * levels + k, self.running[b], self.terms)

        def close(self):
            terms = self.terms
            for b in range(OCEAN_REGIONS):
                here = self.in_basin[b]
                heat = over_longitude(jnp.where(here, self.heat_sum, 0.0))
                terms = jnp.where(lane == HEAT + b, heat, terms)
                flux = over_longitude(jnp.where(here, self.flux, 0.0))
                terms = jnp.where(lane == FLUX + b, flux, terms)
            terms = jnp.where(lane == MEAN, over_longitude(self.mean_sum), terms)
            terms = jnp.where(lane == WET, over_longitude(self.wet_sum), terms)
            parcel[2 * self.block, TERMS : TERMS + 8, :] = terms
            parcel[2 * self.block + 1, TERMS : TERMS + 8, :] = pltpu.roll(terms, 4, 0)

    products = Products(width)

    def rows_of(parts, block, fill):
        sums = []
        for r in range(ROWS):
            spread = lambda q, k, count: jnp.broadcast_to(
                parts[q, k, r : r + 1, :], (count, width)
            )
            sums.append(products.row(spread, levels))
            for k in range(r * levels // ROWS, (r + 1) * levels // ROWS):
                fill.level(k)
        for pair in range(ROWS // 2):
            parcel[2 * block + pair // 2, 8 * (pair % 2) : 8 * (pair % 2) + 8, :] = class_tile(
                sums[2 * pair], sums[2 * pair + 1]
            )
        fill.close()

    for copy in planes:
        copy.wait()
    field_copy(0, 0).wait()
    field_copy(1, 0).wait()
    opening = Block(jnp.int32(0), even)
    for k in range(levels):
        opening.level(k)
    opening.close()

    def two_blocks(i, carry):
        @pl.when(i < chunks - 1)
        def _():
            field_copy(0, i + 1).wait()
            field_copy(1, i + 1).wait()

        rows_of(even, 2 * i, Block(2 * i + 1, odd))
        rows_of(odd, 2 * i + 1, Block(jnp.minimum(2 * i + 2, blocks - 1), even))
        return carry

    lax.fori_loop(0, chunks, two_blocks, 0)

    final = parallels - 1
    half = width // 2
    span = zonal[final : final + 1, :]
    for k in range(levels):
        last[LAST_THETA + k : LAST_THETA + k + 1, :] = theta[k, final : final + 1, :]
        last[LAST_VOLUME + k : LAST_VOLUME + k + 1, :] = tier[k] * span
        last[LAST_SPEED + k : LAST_SPEED + k + 1, :] = speed[k, final : final + 1, :]
    north_depth = depth[final : final + 1, :].astype(jnp.float32)
    last[LAST_DEPTH : LAST_DEPTH + 1, :] = north_depth
    last[LAST_LABEL : LAST_LABEL + 1, :] = label[final : final + 1, :].astype(jnp.float32)
    last[LAST_LABEL + 1 :, :] = jnp.zeros((LAST_ROWS - LAST_LABEL - 1, width), jnp.float32)
    totals = jnp.zeros((ROWS, LANES), jnp.float32)
    for d in range(0, 2 * blocks, 2):
        totals = totals + parcel[d, TERMS : TERMS + 8, :]
    totals = jnp.sum(totals, axis=0, keepdims=True)
    north = last[LAST_THETA : LAST_THETA + levels, :]
    for d in range(2 * blocks):
        parcel[d, DEPTHS : DEPTHS + 1, :] = north_depth[:, :half]
        parcel[d, DEPTHS + 1 : DEPTHS + 2, :] = north_depth[:, half:]
        parcel[d, TOTALS : TOTALS + 1, :] = totals
        parcel[d, TOTALS + 1 : TOTALS + 2, :] = jnp.zeros((1, LANES), jnp.float32)
        parcel[d, EDGES : EDGES + levels, :] = north[:, :half]
        parcel[d, EDGES + levels : EDGES + 2 * levels, :] = north[:, half:]


def last_kernel(where_to, parcels, last, halo, share, parts, edge):
    levels = EDGE - 8
    width = last.shape[1]
    devices = parcels.shape[0]
    total = parcels[0, 0:EDGES, :]
    for d in range(1, devices):
        total = total + parcels[d, 0:EDGES, :]
    columns = []
    for n in range(2):
        source = where_to[n]
        for h in range(2):
            columns.append(
                jnp.concatenate(
                    [
                        parcels[source, EDGES + h * levels : EDGES + (h + 1) * levels, :],
                        parcels[source, DEPTHS + h : DEPTHS + h + 1, :],
                        jnp.zeros((EDGE - levels - 1, LANES), jnp.float32),
                    ],
                    axis=0,
                )
            )
    columns = jnp.concatenate(columns, axis=1)
    high, rest = split_in_two(columns)
    middle, lowest = split_in_two(rest)
    source = lax.broadcasted_iota(jnp.int32, (2 * width, width), 0)
    target = lax.broadcasted_iota(jnp.int32, (2 * width, width), 1)
    mirror = jnp.where(source + target == where_to[2] + (width - 1), 1.0, 0.0).astype(jnp.bfloat16)
    pieces = jnp.dot(
        jnp.concatenate([high, middle, lowest], axis=0).astype(jnp.bfloat16),
        mirror,
        preferred_element_type=jnp.float32,
    )
    folded = pieces[0:EDGE] + pieces[EDGE : 2 * EDGE] + pieces[2 * EDGE : 3 * EDGE]
    edge[...] = jnp.where(where_to[3] == 1, folded, halo[...])

    own = last[LAST_THETA : LAST_THETA + levels, :]
    face = 0.5 * (own + edge[0:levels, :])
    face_depth = jnp.minimum(last[LAST_DEPTH : LAST_DEPTH + 1, :], edge[levels : levels + 1, :])
    level_id = lax.broadcasted_iota(jnp.int32, own.shape, 0).astype(jnp.float32)
    volume = jnp.where(
        level_id < jnp.broadcast_to(face_depth, own.shape),
        last[LAST_VOLUME : LAST_VOLUME + levels, :],
        0.0,
    )
    transport = volume * last[LAST_SPEED : LAST_SPEED + levels, :]
    basin = jnp.broadcast_to(last[LAST_LABEL : LAST_LABEL + 1, :], own.shape)
    for q, value in enumerate(interpolation(face, transport, basin * float(HIGH))):
        parts[q] = value
    sums = Products(width).row(
        lambda q, k, count: jnp.broadcast_to(parts[q, k : k + 1, :], (count, width)), levels
    )
    last_class = class_tile(sums, jnp.zeros_like(sums))

    lane = lax.broadcasted_iota(jnp.int32, (levels, LANES), 1)
    below = lax.broadcasted_iota(jnp.int32, (levels, LANES), 0) <= lane % levels
    heat = transport * face
    everything = lambda x: over_longitude(jnp.sum(x, axis=0, keepdims=True))
    running = jnp.zeros((levels, LANES), jnp.float32)
    lane1 = lane[0:1]
    terms = jnp.zeros((1, LANES), jnp.float32)
    for b in range(OCEAN_REGIONS):
        here = basin == float(b)
        level_sum = over_longitude(jnp.where(here, transport, 0.0))
        running = jnp.where((lane // levels == b) & below, level_sum, running)
        terms = jnp.where(lane1 == HEAT + b, everything(jnp.where(here, heat, 0.0)), terms)
    terms = jnp.where(lane1 == MEAN, everything(volume * face), terms)
    terms = jnp.where(lane1 == WET, everything(volume), terms)
    terms = terms + jnp.sum(running, axis=0, keepdims=True)

    place_id = lax.broadcasted_iota(jnp.int32, (EDGE, LANES), 0)
    lane24 = lax.broadcasted_iota(jnp.int32, (EDGE, LANES), 1)
    wanted = jnp.where(
        place_id < 16, (place_id & 1) * OCEAN_REGIONS + (place_id >> 2), place_id - 16
    )
    of_place = wanted == (lane24 >> 4)
    from_pair = jnp.where(place_id < 16, (place_id >> 1) & 1, 2)
    tiles = (total[0:8], total[8:16], last_class)
    wide = []
    for low in range(LOW):
        row = jnp.zeros((EDGE, LANES), jnp.float32)
        for n, tile in enumerate(tiles):
            row = jnp.where(
                of_place & (from_pair == n),
                jnp.broadcast_to(tile[low : low + 1], (EDGE, LANES)),
                row,
            )
        wide.append(row)
    wide_high, wide_low = split_in_two(jnp.concatenate(wide, axis=1))
    from_id = lax.broadcasted_iota(jnp.int32, (LANES, LANES), 0)
    to_id = lax.broadcasted_iota(jnp.int32, (LANES, LANES), 1)
    goal = (from_id & (HIGH - 1)) * LOW
    placing = jnp.concatenate(
        [jnp.where(to_id == goal + low, 1.0, 0.0) for low in range(LOW)], axis=0
    ).astype(jnp.bfloat16)
    placed = jnp.dot(
        jnp.concatenate([wide_high, wide_low], axis=0).astype(jnp.bfloat16),
        placing,
        preferred_element_type=jnp.float32,
    )
    placed = placed[0:EDGE] + placed[EDGE : 2 * EDGE]
    share[0:16, :] = placed[0:16]
    share[TERMS : TERMS + 4, :] = total[TERMS : TERMS + 4]
    share[LAST : LAST + 4, :] = placed[16:20]
    share[LAST_TERMS : LAST_TERMS + 1, :] = terms
    share[LAST_TERMS + 1 :, :] = jnp.zeros((SHARE - LAST_TERMS - 1, LANES), jnp.float32)


def finish_kernel(unit_scale, implied_scale, where_to, shares, class_out, stream, heat, implied):
    devices = shares.shape[0]
    rows = 4 * devices
    levels = stream.shape[1]
    mine = shares[0, LAST:SHARE, :]
    for d in range(1, devices):
        mine = mine + shares[d, LAST:SHARE, :]
    for b in range(OCEAN_REGIONS):
        for d in range(devices):
            class_out[b, 4 * d : 4 * d + 4, :] = unit_scale * shares[d, 4 * b : 4 * b + 4, :]
        class_out[b, rows - 1 : rows, :] += unit_scale * mine[b : b + 1]
    terms = jnp.concatenate([shares[d, TERMS : TERMS + 4, :] for d in range(devices)], axis=0)
    row_id = lax.broadcasted_iota(jnp.int32, terms.shape, 0)
    own_terms = mine[LAST_TERMS - LAST : LAST_TERMS - LAST + 1]
    terms = terms + jnp.where(row_id == rows - 1, jnp.broadcast_to(own_terms, terms.shape), 0.0)
    turned = jnp.transpose(
        jnp.concatenate([terms, jnp.zeros((LANES - rows, LANES), jnp.float32)], axis=0)
    )
    for b in range(OCEAN_REGIONS):
        stream[b] = unit_scale * turned[b * levels : (b + 1) * levels, :rows]
    lane = lax.broadcasted_iota(jnp.int32, (1, LANES), 1)
    row_mean = turned[MEAN : MEAN + 1] / jnp.where(lane < rows, turned[WET : WET + 1], 1.0)
    offsets = jnp.zeros((1, LANES), jnp.float32)
    for d in range(devices):
        offsets += jnp.where(d < where_to[4], shares[d, SHARE - 1 : SHARE, :], 0.0)
    for b in range(OCEAN_REGIONS):
        total = turned[(b + 1) * levels - 1 : (b + 1) * levels]
        out = unit_scale / 16.0 * (turned[HEAT + b : HEAT + b + 1] - total * row_mean)
        heat[b : b + 1, :] = out[:, :rows]
        flux = turned[FLUX + b : FLUX + b + 1]
        offset = over_longitude(jnp.where(lane == FLUX + b, offsets, 0.0))
        shift = 1
        while shift < rows:
            flux = flux + jnp.where(lane >= shift, pltpu.roll(flux, shift, 1), 0.0)
            shift *= 2
        implied[b : b + 1, :] = (implied_scale * (flux + offset))[:, :rows]


def exchanged(pieces, axis):
    return lax.all_to_all(pieces, axis, split_axis=0, concat_axis=0, tiled=True)


def body(
    meridional_speed,
    theta_field,
    tier_vertical_span,
    grid_zonal_span,
    grid_plan_extent,
    ocean_energy_input,
    ocean_tier_tally,
    grid_region_label,
    seam_matching_meridian,
):
    levels, parallels, width = theta_field.shape
    lon_size = lax.axis_size("lon")
    lat_size = lax.axis_size("lat")
    lat_index = lax.axis_index("lat")
    width_total = width * lon_size
    unit_scale = math.sqrt(THERMAL_BINS / (width_total * levels))
    implied_scale = 2.0 / math.sqrt(width_total * parallels * lat_size)
    blocks = parallels // ROWS
    chunks = parallels // CHUNK

    southernmost = jnp.concatenate(
        [
            theta_field[:, 0, :],
            ocean_tier_tally[0][None].astype(jnp.float32),
            jnp.zeros((EDGE - levels - 1, width), jnp.float32),
        ]
    )
    halo = lax.ppermute(southernmost, "lat", [(i + 1, i) for i in range(lat_size - 1)])

    start = (seam_matching_meridian[0] + (width_total - (width - 1))) % width_total
    first = start // width
    where_to = jnp.stack(
        [
            first,
            (first + 1) % lon_size,
            start % width,
            (lat_index == lat_size - 1).astype(jnp.int32),
            lat_index.astype(jnp.int32),
        ]
    )

    in_smem = pl.BlockSpec(memory_space=pltpu.SMEM)
    in_vmem = pl.BlockSpec(memory_space=pltpu.VMEM)
    anywhere = pl.BlockSpec(memory_space=pl.ANY)
    plane_f32 = pltpu.VMEM((parallels, width), jnp.float32)
    plane_i32 = pltpu.VMEM((parallels, width), jnp.int32)
    field = pltpu.VMEM((levels, parallels, width), jnp.float32)
    parts = pltpu.VMEM((6, levels, ROWS, width), jnp.float32)
    parcels, last = pl.pallas_call(
        rows_kernel,
        in_specs=[anywhere, anywhere, in_smem] + [anywhere] * 5,
        out_specs=(in_vmem, in_vmem),
        out_shape=(
            jax.ShapeDtypeStruct((2 * blocks, PARCEL, LANES), jnp.float32),
            jax.ShapeDtypeStruct((LAST_ROWS, width), jnp.float32),
        ),
        scratch_shapes=[
            field,
            field,
            plane_f32,
            plane_f32,
            plane_f32,
            plane_i32,
            plane_i32,
            parts,
            parts,
            pltpu.SemaphoreType.DMA((2, chunks)),
            pltpu.SemaphoreType.DMA((5,)),
        ],
        cost_estimate=pl.CostEstimate(
            flops=8_000_000_000, bytes_accessed=4_000_000, transcendentals=0
        ),
        name="rows",
    )(
        theta_field,
        meridional_speed,
        tier_vertical_span,
        grid_zonal_span,
        grid_plan_extent,
        ocean_energy_input,
        ocean_tier_tally,
        grid_region_label,
    )
    received = exchanged(parcels, "lon")
    row_flux = jnp.sum(received[:, TOTALS, :], axis=0)[None]
    turned = [
        (s * lon_size + r, r * lon_size + s) for s in range(lat_size) for r in range(lon_size)
    ]
    of_block = lax.ppermute(row_flux, ("lon", "lat"), turned)
    share = pl.pallas_call(
        last_kernel,
        in_specs=[in_smem, in_vmem, in_vmem, in_vmem],
        out_specs=in_vmem,
        out_shape=jax.ShapeDtypeStruct((SHARE, LANES), jnp.float32),
        scratch_shapes=[
            pltpu.VMEM((6, levels, width), jnp.float32),
            pltpu.VMEM((EDGE, width), jnp.float32),
        ],
        cost_estimate=pl.CostEstimate(
            flops=1_000_000_000, bytes_accessed=600_000, transcendentals=0
        ),
        name="last_row",
    )(where_to, received, last, halo)
    share = jnp.concatenate([share[: SHARE - 1], of_block])
    shares = exchanged(jnp.broadcast_to(share, (lon_size, SHARE, LANES)), "lon")
    class_out, stream, heat, implied = pl.pallas_call(
        functools.partial(finish_kernel, unit_scale, implied_scale),
        in_specs=[in_smem, in_vmem],
        out_specs=(in_vmem,) * 4,
        out_shape=(
            jax.ShapeDtypeStruct((OCEAN_REGIONS, parallels, THERMAL_BINS), jnp.float32),
            jax.ShapeDtypeStruct((OCEAN_REGIONS, levels, parallels), jnp.float32),
            jax.ShapeDtypeStruct((OCEAN_REGIONS, parallels), jnp.float32),
            jax.ShapeDtypeStruct((OCEAN_REGIONS, parallels), jnp.float32),
        ),
        name="finish",
    )(where_to, shares)
    return class_out, jnp.transpose(stream, (0, 2, 1)), heat, implied


def solution(mesh):
    in_specs = (
        P(None, "lat", "lon"),
        P(None, "lat", "lon"),
        P(),
        P("lat", "lon"),
        P("lat", "lon"),
        P("lat", "lon"),
        P("lat", "lon"),
        P("lat", "lon"),
        P("lon"),
    )
    out_specs = (P(None, "lat", None), P(None, "lat", None), P(None, "lat"), P(None, "lat"))
    return jax.shard_map(body, mesh=mesh, in_specs=in_specs, out_specs=out_specs, check_vma=False)
```

time: 322 us -> 61.3 us (0.19)
  matrix products: 210 us -> 0 us
  waiting for transfers between devices: 45.3 us -> 7.39 us
  starting transfers between devices: 30.5 us -> 11.6 us
  Pallas kernels: 0 us -> 18.3 us
  local copies, waits for them, and re-layouts: 20.7 us -> 2.72 us
  blocking collectives: 0 us -> 17.4 us
  other arithmetic: 11.5 us -> 1.53 us
    dot_general x11 -> x0, matrix products: 210 us -> none  [the longest x8 207 us: one_block(): jnp.einsum('bkri,krim->brm', weighted, tent, precision=lax.Precision.HIGH...]
    all_to_all x4 -> x1, waiting for transfers between devices: 45.3 us -> 5.25 us  [exchanged(): return lax.all_to_all(pieces, axis, split_axis=0, concat_axis=0, tiled=True)]
    all_to_all x4 -> x1, starting transfers between devices: 26.7 us -> 7.05 us  [exchanged(): return lax.all_to_all(pieces, axis, split_axis=0, concat_axis=0, tiled=True)]
    pallas_call x0 -> x3, Pallas kernels: none -> 18.3 us  [the longest x1 13.7 us: body(): pl.pallas_call(rows_kernel, in_specs=[anywhere, anywhere, in_smem] + [any...]
    all_to_all x0 -> x1, blocking collectives: none -> 17.4 us  [exchanged(): return lax.all_to_all(pieces, axis, split_axis=0, concat_axis=0, tiled=True)]
    broadcast_in_dim x5 -> x2, local copies, waits for them, and re-layouts: 4.67 us -> 0.02 us  [the longest x1 0.02 us: body(): shares = exchanged(jnp.broadcast_to(share, (lon_size, SHARE, LANES)), 'lon')]
    reduce_sum x4 -> x1, other arithmetic: 4.18 us -> 0.03 us  [body(): row_flux = jnp.sum(received[:, TOTALS, :], axis=0)[None]]
    gather x2 -> x0, local copies, waits for them, and re-layouts: 4.03 us -> none  [the longest x1 2.31 us: body(): reflected_theta = jnp.take(seam_theta, seam_matching_meridian, axis=1)]
  transfers between devices with their start and end apart: 6 -> 3, of which waited for: 3 -> 2; matrix products, arithmetic and copies ran while one was open for 5% -> 5% of each run, Pallas kernels for 0% -> 4%
where the time goes in v2:
time: 61.3 us; the launch traced here: 60.3 us
  Pallas kernels  18.3 us (30%)
  blocking collectives  17.4 us (28%)
  starting transfers between devices  11.6 us (19%)
  waiting for transfers between devices  7.39 us (12%)
  local copies, waits for them, and re-layouts  2.72 us (4%)
  other arithmetic  1.53 us (2%)
  between operations  1.44 us (2%)
    all_to_all x1, blocking collectives, exchanged(): return lax.all_to_all(pieces, axis, split_axis=0, concat_axis=0, tiled=True)  17.4 us
    pallas_call x1, Pallas kernels, body(): pl.pallas_call(rows_kernel, in_specs=[anywhere, anywhere, in_smem] + [any...  13.7 us
    all_to_all x1, starting transfers between devices, exchanged(): return lax.all_to_all(pieces, axis, split_axis=0, concat_axis=0, tiled=True)  7.05 us
    all_to_all x1, waiting for transfers between devices, exchanged(): return lax.all_to_all(pieces, axis, split_axis=0, concat_axis=0, tiled=True)  5.25 us
    ppermute x1, starting transfers between devices, body(): of_block = lax.ppermute(row_flux, ('lon', 'lat'), turned)  2.6 us
    pallas_call x1, Pallas kernels, body(): pl.pallas_call(last_kernel, in_specs=[in_smem, in_vmem, in_vmem, in_vmem]...  2.49 us
    ppermute x1, waiting for transfers between devices, body(): of_block = lax.ppermute(row_flux, ('lon', 'lat'), turned)  2.14 us
    pallas_call x1, Pallas kernels, body(): pl.pallas_call(functools.partial(finish_kernel, unit_scale, implied_scale...  2.08 us
  transfers between devices with their start and end apart: 3, of which 2 were waited for; matrix products, arithmetic and copies ran while one was open for 5% of the time, Pallas kernels for 4%

profile of v2, /device:TPU:32, one launch (start us, length us, event | category | flops | bytes accessed | tf_op | source)
XLA Modules:
  0.0 60.3 jit_solution(5587798577864763932)
XLA Ops:
  0.6 13.7 %rows.1 = (f32[16,56,128]{2,1,0:T(8,128)}, f32[56,256]{1,0:T(8,128)}) custom-call(f32[16,64,256]{2,1,0:T(8,128)} %theta_hbm.1, f32[16,64,256]{2,1,0:T(8,128)} %speed_hbm.1, f32[16]{0:T(128)} %tier.1, f32[64,256]{1,0:T(8,128)} %zonal_hbm.1, f32[64,256]{1,0:T(8,128)} %plan_hbm.1, f32[64,256]{1,0:T(8,128)} %energy_hbm.1, s32[64,256]{1,0:T(8,128)} %depth_hbm.1, ...), custom_call_target="tpu_custom_call" | custom-call | flops 8000000000 | bytes 4000000 | tf_op jit(solution)/shard_map/rows/pallas_call | solution.py:475
  14.4 7.1 %all-to-all-start = ((f32[16,56,128]{2,1,0:T(8,128)}), f32[16,56,128]{2,1,0:T(8,128)S(1)}, u32[]{:S(2)}, u32[]{:S(2)}) async-start(f32[16,56,128]{2,1,0:T(8,128)} %get-tuple-element.10), calls=%async_computation | async-start | bytes 917504 | tf_op jit(solution)/shard_map/all_to_all | solution.py:423
  21.4 0.9 %slice.16 = f32[16,1,256]{2,1,0:T(1,128)S(1)} slice(f32[16,64,256]{2,1,0:T(8,128)} %theta_hbm.1), slice={[0:16], [0:1], [0:256]} | slice | bytes 32768 | tf_op jit(solution)/shard_map/slice | solution.py:449
  22.4 0.1 pad.4.clone
  22.4 0.7 %slice_convert_fusion = f32[1,256]{1,0:T(1,128)S(1)} fusion(s32[64,256]{1,0:T(8,128)} %depth_hbm.1), kind=kLoop, calls=%fused_computation.4 | loop fusion | flops 256 | bytes 2048 | tf_op jit(solution)/shard_map/convert_element_type | solution.py:450
  23.1 0.0 copy-start.2
  23.1 0.1 maximum_maximum_fusion
  23.2 1.9 %collective-permute-start = (f32[24,256]{1,0:T(8,128)S(1)}, f32[24,256]{1,0:T(8,128)S(1)}, u32[]{:S(2)}, u32[]{:S(2)}) collective-permute-start(f32[24,256]{1,0:T(8,128)S(1)} %maximum_maximum_fusion), channel_id=1, source_target_pairs={{1,0},{2,1},{3,2},{4,3},{5,4},{6,5},{7,6},{8,7},{9,8},{10,9},{11,1... | collective-permute-start | bytes 73736 | tf_op jit(solution)/shard_map/ppermute | solution.py:454
  25.1 0.0 copy-done.2
  25.2 0.5 slice.15
  26.4 0.6 stack.27.where_to
  27.0 5.3 %all-to-all-done.parcels = f32[16,56,128]{2,1,0:T(8,128)S(1)} async-done(((f32[16,56,128]{2,1,0:T(8,128)}), f32[16,56,128]{2,1,0:T(8,128)S(1)}, u32[]{:S(2)}, u32[]{:S(2)}) %all-to-all-start) | async-done | bytes 458784 | tf_op jit(solution)/shard_map/all_to_all | solution.py:423
  32.2 0.0 copy-start
  32.3 2.6 %collective-permute-start.1 = (f32[1,128]{1,0:T(1,128)S(1)}, f32[1,128]{1,0:T(1,128)S(1)}, u32[]{:S(2)}, u32[]{:S(2)}) collective-permute-start(f32[1,128]{1,0:T(1,128)S(1)} %bitcast.14), channel_id=1, source_target_pairs={{0,0},{1,16},{2,32},{3,48},{4,64},{5,80},{6,96},{7,112},{8,128},{9... | collective-permute-start | bytes 1544 | tf_op jit(solution)/shard_map/ppermute | solution.py:515
  34.9 0.0 collective-permute-done.halo
  34.9 0.0 copy-start.1
  34.9 0.0 copy-done
  34.9 0.6 copy-done.1
  35.5 2.5 %last_row.1 = f32[32,128]{1,0:T(8,128)} custom-call(s32[5]{0:T(128)} %stack.27.where_to, f32[16,56,128]{2,1,0:T(8,128)} %copy-done, f32[56,256]{1,0:T(8,128)} %get-tuple-element.11.last, f32[24,256]{1,0:T(8,128)} %copy-done.1), custom_call_target="tpu_custom_call" | custom-call | flops 1000000000 | bytes 600000 | tf_op jit(solution)/shard_map/last_row/pallas_call | solution.py:516
  38.0 2.1 %collective-permute-done.1 = f32[1,128]{1,0:T(1,128)S(1)} collective-permute-done((f32[1,128]{1,0:T(1,128)S(1)}, f32[1,128]{1,0:T(1,128)S(1)}, u32[]{:S(2)}, u32[]{:S(2)}) %collective-permute-start.1) | collective-permute-done | bytes 544 | tf_op jit(solution)/shard_map/ppermute | solution.py:515
  40.1 0.7 %pad_maximum_fusion = f32[32,128]{1,0:T(8,128)S(1)} fusion(f32[1,128]{1,0:T(1,128)S(1)} %collective-permute-done.1, f32[31,128]{1,0:T(8,128)} %bitcast.13), kind=kLoop, calls=%fused_computation.1 | loop fusion | flops 4096 | bytes 32768 | tf_op jit(solution)/shard_map/concatenate | solution.py:530
  40.9 17.4 %all_to_all.10.shares = f32[16,32,128]{2,1,0:T(8,128)} all-to-all(f32[16,32,128]{2,1,0:T(8,128)S(1)} %broadcast_in_dim.11), channel_id=1, replica_groups=mesh['lon'=16,'lat'=16] {'lon'}, dimensions={0} | all-to-all | bytes 524288 | tf_op jit(solution)/shard_map/all_to_all | solution.py:423
  58.3 2.1 %finish.1 = (f32[4,64,128]{2,1,0:T(8,128)}, f32[4,16,64]{2,1,0:T(8,128)}, f32[4,64]{1,0:T(4,128)}, f32[4,64]{1,0:T(4,128)}) custom-call(s32[5]{0:T(128)} %stack.27.where_to, f32[16,32,128]{2,1,0:T(8,128)} %all_to_all.10.shares), custom_call_target="tpu_custom_call" | custom-call | tf_op jit(solution)/shard_map/finish/pallas_call | solution.py:532
  (4 shorter events, 0.1 us)
Async XLA Ops:
  14.4 17.8 %all-to-all-start = ((f32[16,56,128]{2,1,0:T(8,128)}), f32[16,56,128]{2,1,0:T(8,128)S(1)}, u32[]{:S(2)}, u32[]{:S(2)}) async-start(f32[16,56,128]{2,1,0:T(8,128)} %get-tuple-element.10), calls=%async_computation | async-start | bytes 917504 | tf_op jit(solution)/shard_map/all_to_all | solution.py:423
  23.1 2.0 %copy-start.2 = (s32[256]{0:T(256)S(1)}, s32[256]{0:T(256)}, u32[]{:S(2)}) copy-start(s32[256]{0:T(256)} %param.17) | copy-start | bytes 3076
  23.2 11.6 %collective-permute-start = (f32[24,256]{1,0:T(8,128)S(1)}, f32[24,256]{1,0:T(8,128)S(1)}, u32[]{:S(2)}, u32[]{:S(2)}) collective-permute-start(f32[24,256]{1,0:T(8,128)S(1)} %maximum_maximum_fusion), channel_id=1, source_target_pairs={{1,0},{2,1},{3,2},{4,3},{5,4},{6,5},{7,6},{8,7},{9,8},{10,9},{11,1... | collective-permute-start | bytes 73736 | tf_op jit(solution)/shard_map/ppermute | solution.py:454
  32.2 2.7 %copy-start = (f32[16,56,128]{2,1,0:T(8,128)}, f32[16,56,128]{2,1,0:T(8,128)S(1)}, u32[]{:S(2)}) copy-start(f32[16,56,128]{2,1,0:T(8,128)S(1)} %all-to-all-done.parcels) | copy-start | bytes 1376260
  32.3 7.9 %collective-permute-start.1 = (f32[1,128]{1,0:T(1,128)S(1)}, f32[1,128]{1,0:T(1,128)S(1)}, u32[]{:S(2)}, u32[]{:S(2)}) collective-permute-start(f32[1,128]{1,0:T(1,128)S(1)} %bitcast.14), channel_id=1, source_target_pairs={{0,0},{1,16},{2,32},{3,48},{4,64},{5,80},{6,96},{7,112},{8,128},{9... | collective-permute-start | bytes 1544 | tf_op jit(solution)/shard_map/ppermute | solution.py:515
  34.9 0.6 %copy-start.1 = (f32[24,256]{1,0:T(8,128)}, f32[24,256]{1,0:T(8,128)S(1)}, u32[]{:S(2)}) copy-start(f32[24,256]{1,0:T(8,128)S(1)} %collective-permute-done.halo) | copy-start | bytes 73732

commit v3 on v2

--- a/solution.py
+++ b/solution.py
@@ -405,7 +405,7 @@
     row_mean = turned[MEAN : MEAN + 1] / jnp.where(lane < rows, turned[WET : WET + 1], 1.0)
     offsets = jnp.zeros((1, LANES), jnp.float32)
     for d in range(devices):
-        offsets += jnp.where(d < where_to[4], shares[d, SHARE - 1 : SHARE, :], 0.0)
+        offsets += shares[d, SHARE - 1 : SHARE, :]
     for b in range(OCEAN_REGIONS):
         total = turned[(b + 1) * levels - 1 : (b + 1) * levels]
         out = unit_scale / 16.0 * (turned[HEAT + b : HEAT + b + 1] - total * row_mean)
@@ -509,10 +509,12 @@
     )
     received = exchanged(parcels, "lon")
     row_flux = jnp.sum(received[:, TOTALS, :], axis=0)[None]
-    turned = [
-        (s * lon_size + r, r * lon_size + s) for s in range(lat_size) for r in range(lon_size)
+    northward = [
+        (r * lat_size + s, r * lat_size + s + r)
+        for r in range(1, lon_size)
+        for s in range(lat_size - r)
     ]
-    of_block = lax.ppermute(row_flux, ("lon", "lat"), turned)
+    of_block = lax.ppermute(row_flux, ("lon", "lat"), northward)
     share = pl.pallas_call(
         last_kernel,
         in_specs=[in_smem, in_vmem, in_vmem, in_vmem],

time: 61.3 us -> 58.3 us (0.951)
  waiting for transfers between devices: 7.39 us -> 5.26 us
  starting transfers between devices: 11.6 us -> 9.61 us
  blocking collectives: 17.4 us -> 19 us
    ppermute x1, waiting for transfers between devices: 2.14 us -> 0.01 us  [body(): of_block = lax.ppermute(row_flux, ('lon', 'lat'), northward)]
    ppermute x1, starting transfers between devices: 2.6 us -> 0.65 us  [body(): of_block = lax.ppermute(row_flux, ('lon', 'lat'), northward)]
    all_to_all x1, blocking collectives: 17.4 us -> 19 us  [exchanged(): return lax.all_to_all(pieces, axis, split_axis=0, concat_axis=0, tiled=True)]
  transfers between devices with their start and end apart: 3 -> 3, of which waited for: 2 -> 1; matrix products, arithmetic and copies ran while one was open for 5% -> 5% of each run, Pallas kernels for 4% -> 4%
where the time goes in v3:
time: 58.3 us; the launch traced here: 57.8 us
  blocking collectives  19 us (33%)
  Pallas kernels  18.3 us (31%)
  starting transfers between devices  9.61 us (16%)
  waiting for transfers between devices  5.26 us (9%)
  local copies, waits for them, and re-layouts  2.73 us (5%)
  other arithmetic  1.53 us (3%)
  between operations  1.43 us (2%)
    all_to_all x1, blocking collectives, exchanged(): return lax.all_to_all(pieces, axis, split_axis=0, concat_axis=0, tiled=True)  19 us
    pallas_call x1, Pallas kernels, body(): pl.pallas_call(rows_kernel, in_specs=[anywhere, anywhere, in_smem] + [any...  13.7 us
    all_to_all x1, starting transfers between devices, exchanged(): return lax.all_to_all(pieces, axis, split_axis=0, concat_axis=0, tiled=True)  7.05 us
    all_to_all x1, waiting for transfers between devices, exchanged(): return lax.all_to_all(pieces, axis, split_axis=0, concat_axis=0, tiled=True)  5.25 us
    pallas_call x1, Pallas kernels, body(): pl.pallas_call(last_kernel, in_specs=[in_smem, in_vmem, in_vmem, in_vmem]...  2.49 us
    pallas_call x1, Pallas kernels, body(): pl.pallas_call(functools.partial(finish_kernel, unit_scale, implied_scale...  2.08 us
    ppermute x1, starting transfers between devices, body(): lax.ppermute(southernmost, 'lat', [(i + 1, i) for i in range(lat_size - 1)])  1.91 us
  transfers between devices with their start and end apart: 3, of which 1 were waited for; matrix products, arithmetic and copies ran while one was open for 5% of the time, Pallas kernels for 4%

profile of v3, /device:TPU:32, one launch (start us, length us, event | category | flops | bytes accessed | tf_op | source)
XLA Modules:
  0.0 57.8 jit_solution(10100977802059680211)
XLA Ops:
  0.6 13.7 %rows.1 = (f32[16,56,128]{2,1,0:T(8,128)}, f32[56,256]{1,0:T(8,128)}) custom-call(f32[16,64,256]{2,1,0:T(8,128)} %theta_hbm.1, f32[16,64,256]{2,1,0:T(8,128)} %speed_hbm.1, f32[16]{0:T(128)} %tier.1, f32[64,256]{1,0:T(8,128)} %zonal_hbm.1, f32[64,256]{1,0:T(8,128)} %plan_hbm.1, f32[64,256]{1,0:T(8,128)} %energy_hbm.1, s32[64,256]{1,0:T(8,128)} %depth_hbm.1, ...), custom_call_target="tpu_custom_call" | custom-call | flops 8000000000 | bytes 4000000 | tf_op jit(solution)/shard_map/rows/pallas_call | solution.py:475
  14.4 7.1 %all-to-all-start = ((f32[16,56,128]{2,1,0:T(8,128)}), f32[16,56,128]{2,1,0:T(8,128)S(1)}, u32[]{:S(2)}, u32[]{:S(2)}) async-start(f32[16,56,128]{2,1,0:T(8,128)} %get-tuple-element.10), calls=%async_computation | async-start | bytes 917504 | tf_op jit(solution)/shard_map/all_to_all | solution.py:423
  21.4 0.9 %slice.16 = f32[16,1,256]{2,1,0:T(1,128)S(1)} slice(f32[16,64,256]{2,1,0:T(8,128)} %theta_hbm.1), slice={[0:16], [0:1], [0:256]} | slice | bytes 32768 | tf_op jit(solution)/shard_map/slice | solution.py:449
  22.4 0.1 pad.4.clone
  22.4 0.7 %slice_convert_fusion = f32[1,256]{1,0:T(1,128)S(1)} fusion(s32[64,256]{1,0:T(8,128)} %depth_hbm.1), kind=kLoop, calls=%fused_computation.4 | loop fusion | flops 256 | bytes 2048 | tf_op jit(solution)/shard_map/convert_element_type | solution.py:450
  23.1 0.0 copy-start.2
  23.1 0.1 maximum_maximum_fusion
  23.2 1.9 %collective-permute-start = (f32[24,256]{1,0:T(8,128)S(1)}, f32[24,256]{1,0:T(8,128)S(1)}, u32[]{:S(2)}, u32[]{:S(2)}) collective-permute-start(f32[24,256]{1,0:T(8,128)S(1)} %maximum_maximum_fusion), channel_id=1, source_target_pairs={{1,0},{2,1},{3,2},{4,3},{5,4},{6,5},{7,6},{8,7},{9,8},{10,9},{11,1... | collective-permute-start | bytes 73736 | tf_op jit(solution)/shard_map/ppermute | solution.py:454
  25.1 0.0 copy-done.2
  25.2 0.5 slice.15
  26.4 0.6 %stack.27.where_to = s32[5]{0:T(128)} concatenate(s32[1]{0:T(128)} %bitcast.1, s32[1]{0:T(128)} %bitcast.2, s32[1]{0:T(128)} %bitcast.3, s32[1]{0:T(128)} %bitcast.4, s32[1]{0:T(128)} %bitcast.5), dimensions={0} | concatenate | bytes 40 | tf_op jit(solution)/shard_map/stack | solution.py:458
  27.0 5.3 %all-to-all-done.parcels = f32[16,56,128]{2,1,0:T(8,128)S(1)} async-done(((f32[16,56,128]{2,1,0:T(8,128)}), f32[16,56,128]{2,1,0:T(8,128)S(1)}, u32[]{:S(2)}, u32[]{:S(2)}) %all-to-all-start) | async-done | bytes 458784 | tf_op jit(solution)/shard_map/all_to_all | solution.py:423
  32.2 0.0 copy-start
  32.3 0.7 %collective-permute-start.1 = (f32[1,128]{1,0:T(1,128)S(1)}, f32[1,128]{1,0:T(1,128)S(1)}, u32[]{:S(2)}, u32[]{:S(2)}) collective-permute-start(f32[1,128]{1,0:T(1,128)S(1)} %bitcast.14), channel_id=1, source_target_pairs={{16,17},{17,18},{18,19},{19,20},{20,21},{21,22},{22,23},{23,24},{2... | collective-permute-start | bytes 1544 | tf_op jit(solution)/shard_map/ppermute | solution.py:517
  32.9 0.0 collective-permute-done.halo
  32.9 0.0 copy-start.1
  32.9 0.1 copy-done
  33.0 0.5 copy-done.1
  33.5 2.5 %last_row.1 = f32[32,128]{1,0:T(8,128)} custom-call(s32[5]{0:T(128)} %stack.27.where_to, f32[16,56,128]{2,1,0:T(8,128)} %copy-done, f32[56,256]{1,0:T(8,128)} %get-tuple-element.11.last, f32[24,256]{1,0:T(8,128)} %copy-done.1), custom_call_target="tpu_custom_call" | custom-call | flops 1000000000 | bytes 600000 | tf_op jit(solution)/shard_map/last_row/pallas_call | solution.py:518
  36.0 0.0 collective-permute-done.1
  36.0 0.7 %pad_maximum_fusion = f32[32,128]{1,0:T(8,128)S(1)} fusion(f32[1,128]{1,0:T(1,128)S(1)} %collective-permute-done.1, f32[31,128]{1,0:T(8,128)} %bitcast.13), kind=kLoop, calls=%fused_computation.1 | loop fusion | flops 4096 | bytes 32768 | tf_op jit(solution)/shard_map/concatenate | solution.py:532
  36.8 19.0 %all_to_all.10.shares = f32[16,32,128]{2,1,0:T(8,128)} all-to-all(f32[16,32,128]{2,1,0:T(8,128)S(1)} %broadcast_in_dim.11), channel_id=1, replica_groups=mesh['lon'=16,'lat'=16] {'lon'}, dimensions={0} | all-to-all | bytes 524288 | tf_op jit(solution)/shard_map/all_to_all | solution.py:423
  55.7 2.1 %finish.1 = (f32[4,64,128]{2,1,0:T(8,128)}, f32[4,16,64]{2,1,0:T(8,128)}, f32[4,64]{1,0:T(4,128)}, f32[4,64]{1,0:T(4,128)}) custom-call(s32[5]{0:T(128)} %stack.27.where_to, f32[16,32,128]{2,1,0:T(8,128)} %all_to_all.10.shares), custom_call_target="tpu_custom_call" | custom-call | tf_op jit(solution)/shard_map/finish/pallas_call | solution.py:534
  (4 shorter events, 0.1 us)
Async XLA Ops:
  14.4 17.8 %all-to-all-start = ((f32[16,56,128]{2,1,0:T(8,128)}), f32[16,56,128]{2,1,0:T(8,128)S(1)}, u32[]{:S(2)}, u32[]{:S(2)}) async-start(f32[16,56,128]{2,1,0:T(8,128)} %get-tuple-element.10), calls=%async_computation | async-start | bytes 917504 | tf_op jit(solution)/shard_map/all_to_all | solution.py:423
  23.1 2.0 %copy-start.2 = (s32[256]{0:T(256)S(1)}, s32[256]{0:T(256)}, u32[]{:S(2)}) copy-start(s32[256]{0:T(256)} %param.17) | copy-start | bytes 3076
  23.2 9.7 %collective-permute-start = (f32[24,256]{1,0:T(8,128)S(1)}, f32[24,256]{1,0:T(8,128)S(1)}, u32[]{:S(2)}, u32[]{:S(2)}) collective-permute-start(f32[24,256]{1,0:T(8,128)S(1)} %maximum_maximum_fusion), channel_id=1, source_target_pairs={{1,0},{2,1},{3,2},{4,3},{5,4},{6,5},{7,6},{8,7},{9,8},{10,9},{11,1... | collective-permute-start | bytes 73736 | tf_op jit(solution)/shard_map/ppermute | solution.py:454
  32.2 0.8 %copy-start = (f32[16,56,128]{2,1,0:T(8,128)}, f32[16,56,128]{2,1,0:T(8,128)S(1)}, u32[]{:S(2)}) copy-start(f32[16,56,128]{2,1,0:T(8,128)S(1)} %all-to-all-done.parcels) | copy-start | bytes 1376260
  32.3 3.8 %collective-permute-start.1 = (f32[1,128]{1,0:T(1,128)S(1)}, f32[1,128]{1,0:T(1,128)S(1)}, u32[]{:S(2)}, u32[]{:S(2)}) collective-permute-start(f32[1,128]{1,0:T(1,128)S(1)} %bitcast.14), channel_id=1, source_target_pairs={{16,17},{17,18},{18,19},{19,20},{20,21},{21,22},{22,23},{23,24},{2... | collective-permute-start | bytes 1544 | tf_op jit(solution)/shard_map/ppermute | solution.py:517
  32.9 0.6 %copy-start.1 = (f32[24,256]{1,0:T(8,128)}, f32[24,256]{1,0:T(8,128)S(1)}, u32[]{:S(2)}) copy-start(f32[24,256]{1,0:T(8,128)S(1)} %collective-permute-done.halo) | copy-start | bytes 73732

commit v4 on v3

--- a/solution.py
+++ b/solution.py
@@ -20,9 +20,11 @@
 GROUPS = OCEAN_REGIONS * HIGH
 LANES = 128
 EDGE = 24
-TERMS, DEPTHS, TOTALS, EDGES, PARCEL = 16, 20, 22, 24, 56
+TERMS, TOTALS, LEVEL, PARCEL = 16, 20, 24, 32
+BASIN_UNIT = 32.0
 LAST, LAST_TERMS, SHARE = 20, 24, 32
-LAST_THETA, LAST_VOLUME, LAST_SPEED, LAST_DEPTH, LAST_LABEL, LAST_ROWS = 0, 16, 32, 48, 49, 56
+SMALL_KERNEL = 8 * 1024 * 1024
+LAST_THETA, LAST_VOLUME, LAST_SPEED, LAST_MARKS, LAST_ROWS = 0, 16, 32, 48, 56
 HEAT, FLUX, MEAN, WET = 64, 68, 76, 77
 
 
@@ -113,6 +115,7 @@
     label_hbm,
     parcel,
     last,
+    south,
     theta,
     speed,
     zonal,
@@ -256,70 +259,88 @@
         last[LAST_THETA + k : LAST_THETA + k + 1, :] = theta[k, final : final + 1, :]
         last[LAST_VOLUME + k : LAST_VOLUME + k + 1, :] = tier[k] * span
         last[LAST_SPEED + k : LAST_SPEED + k + 1, :] = speed[k, final : final + 1, :]
-    north_depth = depth[final : final + 1, :].astype(jnp.float32)
-    last[LAST_DEPTH : LAST_DEPTH + 1, :] = north_depth
-    last[LAST_LABEL : LAST_LABEL + 1, :] = label[final : final + 1, :].astype(jnp.float32)
-    last[LAST_LABEL + 1 :, :] = jnp.zeros((LAST_ROWS - LAST_LABEL - 1, width), jnp.float32)
+    for k in range(levels):
+        south[k : k + 1, :] = theta[k, 0:1, :]
+    south[levels : levels + 1, :] = depth[0:1, :].astype(jnp.float32)
+    south[levels + 1 :, :] = jnp.zeros((EDGE - levels - 1, width), jnp.float32)
+    marks = (depth[final : final + 1, :] + 32 * label[final : final + 1, :]).astype(jnp.float32)
+    last[LAST_MARKS : LAST_MARKS + 1, :] = marks
+    last[LAST_MARKS + 1 :, :] = jnp.zeros((LAST_ROWS - LAST_MARKS - 1, width), jnp.float32)
     totals = jnp.zeros((ROWS, LANES), jnp.float32)
     for d in range(0, 2 * blocks, 2):
         totals = totals + parcel[d, TERMS : TERMS + 8, :]
     totals = jnp.sum(totals, axis=0, keepdims=True)
-    north = last[LAST_THETA : LAST_THETA + levels, :]
     for d in range(2 * blocks):
-        parcel[d, DEPTHS : DEPTHS + 1, :] = north_depth[:, :half]
-        parcel[d, DEPTHS + 1 : DEPTHS + 2, :] = north_depth[:, half:]
         parcel[d, TOTALS : TOTALS + 1, :] = totals
-        parcel[d, TOTALS + 1 : TOTALS + 2, :] = jnp.zeros((1, LANES), jnp.float32)
-        parcel[d, EDGES : EDGES + levels, :] = north[:, :half]
-        parcel[d, EDGES + levels : EDGES + 2 * levels, :] = north[:, half:]
-
-
-def last_kernel(where_to, parcels, last, halo, share, parts, edge):
+        parcel[d, TOTALS + 1 : LEVEL, :] = jnp.zeros((LEVEL - TOTALS - 1, LANES), jnp.float32)
+        for n, q in enumerate((LAST_THETA + d, LAST_VOLUME + d, LAST_SPEED + d, LAST_MARKS)):
+            row = last[q : q + 1, :]
+            parcel[d, LEVEL + 2 * n : LEVEL + 2 * n + 1, :] = row[:, :half]
+            parcel[d, LEVEL + 2 * n + 1 : LEVEL + 2 * n + 2, :] = row[:, half:]
+
+
+def last_kernel(lon_size, lat_size, seam, parcels, last, halo, share, parts):
     levels = EDGE - 8
     width = last.shape[1]
     devices = parcels.shape[0]
-    total = parcels[0, 0:EDGES, :]
+    lon_index = lax.axis_index("lon")
+    at_fold = lax.axis_index("lat") == lat_size - 1
+    start = seam[0] + lon_index * width + (lon_size * width - (width - 1))
+    first, offset = start // width, start % width
+    total = parcels[0, 0:LEVEL, :]
     for d in range(1, devices):
-        total = total + parcels[d, 0:EDGES, :]
-    columns = []
-    for n in range(2):
-        source = where_to[n]
-        for h in range(2):
-            columns.append(
-                jnp.concatenate(
-                    [
-                        parcels[source, EDGES + h * levels : EDGES + (h + 1) * levels, :],
-                        parcels[source, DEPTHS + h : DEPTHS + h + 1, :],
-                        jnp.zeros((EDGE - levels - 1, LANES), jnp.float32),
-                    ],
-                    axis=0,
+        total = total + parcels[d, 0:LEVEL, :]
+
+    def whole_row(n):
+        half = lambda h: jnp.concatenate(
+            [parcels[d, LEVEL + 2 * n + h : LEVEL + 2 * n + h + 1, :] for d in range(devices)], axis=0
+        )
+        return jnp.concatenate([half(0), half(1)], axis=1)
+
+    def mirrored(n):
+        tiles = []
+        for step in range(2):
+            for h in range(2):
+                at = LEVEL + 2 * n + h
+                tiles.append(
+                    jnp.concatenate(
+                        [
+                            parcels[(first + (step - d)) & (devices - 1), at : at + 1, :]
+                            for d in range(devices)
+                        ],
+                        axis=0,
+                    )
                 )
-            )
-    columns = jnp.concatenate(columns, axis=1)
-    high, rest = split_in_two(columns)
+        return jnp.concatenate(tiles, axis=1)
+
+    high, rest = split_in_two(mirrored(0))
     middle, lowest = split_in_two(rest)
+    blocks_marks = mirrored(3)
+    blocks_depth = blocks_marks - BASIN_UNIT * jnp.floor(blocks_marks * (1.0 / BASIN_UNIT))
     source = lax.broadcasted_iota(jnp.int32, (2 * width, width), 0)
     target = lax.broadcasted_iota(jnp.int32, (2 * width, width), 1)
-    mirror = jnp.where(source + target == where_to[2] + (width - 1), 1.0, 0.0).astype(jnp.bfloat16)
+    mirror = jnp.where(source + target == offset + (width - 1), 1.0, 0.0).astype(jnp.bfloat16)
     pieces = jnp.dot(
-        jnp.concatenate([high, middle, lowest], axis=0).astype(jnp.bfloat16),
+        jnp.concatenate([high, middle, lowest, blocks_depth], axis=0).astype(jnp.bfloat16),
         mirror,
         preferred_element_type=jnp.float32,
     )
-    folded = pieces[0:EDGE] + pieces[EDGE : 2 * EDGE] + pieces[2 * EDGE : 3 * EDGE]
-    edge[...] = jnp.where(where_to[3] == 1, folded, halo[...])
-
-    own = last[LAST_THETA : LAST_THETA + levels, :]
-    face = 0.5 * (own + edge[0:levels, :])
-    face_depth = jnp.minimum(last[LAST_DEPTH : LAST_DEPTH + 1, :], edge[levels : levels + 1, :])
-    level_id = lax.broadcasted_iota(jnp.int32, own.shape, 0).astype(jnp.float32)
-    volume = jnp.where(
-        level_id < jnp.broadcast_to(face_depth, own.shape),
-        last[LAST_VOLUME : LAST_VOLUME + levels, :],
-        0.0,
-    )
-    transport = volume * last[LAST_SPEED : LAST_SPEED + levels, :]
-    basin = jnp.broadcast_to(last[LAST_LABEL : LAST_LABEL + 1, :], own.shape)
+    folded = pieces[0:16] + pieces[16:32] + pieces[32:48]
+
+    spread_out = lambda row: jnp.broadcast_to(row, (levels, width))
+    theta = jnp.where(at_fold, whole_row(0), last[LAST_THETA : LAST_THETA + levels, :])
+    full_volume = jnp.where(at_fold, whole_row(1), last[LAST_VOLUME : LAST_VOLUME + levels, :])
+    speed = jnp.where(at_fold, whole_row(2), last[LAST_SPEED : LAST_SPEED + levels, :])
+    marks = jnp.where(at_fold, whole_row(3), spread_out(last[LAST_MARKS : LAST_MARKS + 1, :]))
+    north = jnp.where(at_fold, folded, halo[0:levels, :])
+    north_depth = jnp.where(at_fold, pieces[48:64], spread_out(halo[levels : levels + 1, :]))
+    basin = jnp.floor(marks * (1.0 / BASIN_UNIT))
+    face = 0.5 * (theta + north)
+    face_depth = jnp.minimum(marks - BASIN_UNIT * basin, north_depth)
+    row_id = lax.broadcasted_iota(jnp.int32, (levels, width), 0)
+    level_id = jnp.where(at_fold, lon_index, row_id).astype(jnp.float32)
+    volume = jnp.where(level_id < face_depth, full_volume, 0.0)
+    transport = volume * speed
     for q, value in enumerate(interpolation(face, transport, basin * float(HIGH))):
         parts[q] = value
     sums = Products(width).row(
@@ -328,7 +349,8 @@
     last_class = class_tile(sums, jnp.zeros_like(sums))
 
     lane = lax.broadcasted_iota(jnp.int32, (levels, LANES), 1)
-    below = lax.broadcasted_iota(jnp.int32, (levels, LANES), 0) <= lane % levels
+    own_level = lax.broadcasted_iota(jnp.int32, (levels, LANES), 0)
+    below = jnp.where(at_fold, lon_index, own_level) <= lane % levels
     heat = transport * face
     everything = lambda x: over_longitude(jnp.sum(x, axis=0, keepdims=True))
     running = jnp.zeros((levels, LANES), jnp.float32)
@@ -381,7 +403,7 @@
     share[LAST_TERMS + 1 :, :] = jnp.zeros((SHARE - LAST_TERMS - 1, LANES), jnp.float32)
 
 
-def finish_kernel(unit_scale, implied_scale, where_to, shares, class_out, stream, heat, implied):
+def finish_kernel(unit_scale, implied_scale, shares, class_out, stream, heat, implied):
     devices = shares.shape[0]
     rows = 4 * devices
     levels = stream.shape[1]
@@ -437,33 +459,11 @@
     levels, parallels, width = theta_field.shape
     lon_size = lax.axis_size("lon")
     lat_size = lax.axis_size("lat")
-    lat_index = lax.axis_index("lat")
     width_total = width * lon_size
     unit_scale = math.sqrt(THERMAL_BINS / (width_total * levels))
     implied_scale = 2.0 / math.sqrt(width_total * parallels * lat_size)
     blocks = parallels // ROWS
     chunks = parallels // CHUNK
-
-    southernmost = jnp.concatenate(
-        [
-            theta_field[:, 0, :],
-            ocean_tier_tally[0][None].astype(jnp.float32),
-            jnp.zeros((EDGE - levels - 1, width), jnp.float32),
-        ]
-    )
-    halo = lax.ppermute(southernmost, "lat", [(i + 1, i) for i in range(lat_size - 1)])
-
-    start = (seam_matching_meridian[0] + (width_total - (width - 1))) % width_total
-    first = start // width
-    where_to = jnp.stack(
-        [
-            first,
-            (first + 1) % lon_size,
-            start % width,
-            (lat_index == lat_size - 1).astype(jnp.int32),
-            lat_index.astype(jnp.int32),
-        ]
-    )
 
     in_smem = pl.BlockSpec(memory_space=pltpu.SMEM)
     in_vmem = pl.BlockSpec(memory_space=pltpu.VMEM)
@@ -472,13 +472,14 @@
     plane_i32 = pltpu.VMEM((parallels, width), jnp.int32)
     field = pltpu.VMEM((levels, parallels, width), jnp.float32)
     parts = pltpu.VMEM((6, levels, ROWS, width), jnp.float32)
-    parcels, last = pl.pallas_call(
+    parcels, last, southernmost = pl.pallas_call(
         rows_kernel,
         in_specs=[anywhere, anywhere, in_smem] + [anywhere] * 5,
-        out_specs=(in_vmem, in_vmem),
+        out_specs=(in_vmem,) * 3,
         out_shape=(
             jax.ShapeDtypeStruct((2 * blocks, PARCEL, LANES), jnp.float32),
             jax.ShapeDtypeStruct((LAST_ROWS, width), jnp.float32),
+            jax.ShapeDtypeStruct((EDGE, width), jnp.float32),
         ),
         scratch_shapes=[
             field,
@@ -508,6 +509,7 @@
         grid_region_label,
     )
     received = exchanged(parcels, "lon")
+    halo = lax.ppermute(southernmost, "lat", [(i + 1, i) for i in range(lat_size - 1)])
     row_flux = jnp.sum(received[:, TOTALS, :], axis=0)[None]
     northward = [
         (r * lat_size + s, r * lat_size + s + r)
@@ -516,24 +518,25 @@
     ]
     of_block = lax.ppermute(row_flux, ("lon", "lat"), northward)
     share = pl.pallas_call(
-        last_kernel,
+        functools.partial(last_kernel, lon_size, lat_size),
         in_specs=[in_smem, in_vmem, in_vmem, in_vmem],
         out_specs=in_vmem,
         out_shape=jax.ShapeDtypeStruct((SHARE, LANES), jnp.float32),
         scratch_shapes=[
             pltpu.VMEM((6, levels, width), jnp.float32),
-            pltpu.VMEM((EDGE, width), jnp.float32),
         ],
+        compiler_params=pltpu.CompilerParams(vmem_limit_bytes=SMALL_KERNEL),
         cost_estimate=pl.CostEstimate(
             flops=1_000_000_000, bytes_accessed=600_000, transcendentals=0
         ),
         name="last_row",
-    )(where_to, received, last, halo)
-    share = jnp.concatenate([share[: SHARE - 1], of_block])
+    )(seam_matching_meridian, received, last, halo)
+    row_id = lax.broadcasted_iota(jnp.int32, share.shape, 0)
+    share = jnp.where(row_id == SHARE - 1, of_block, share)
     shares = exchanged(jnp.broadcast_to(share, (lon_size, SHARE, LANES)), "lon")
     class_out, stream, heat, implied = pl.pallas_call(
         functools.partial(finish_kernel, unit_scale, implied_scale),
-        in_specs=[in_smem, in_vmem],
+        in_specs=[in_vmem],
         out_specs=(in_vmem,) * 4,
         out_shape=(
             jax.ShapeDtypeStruct((OCEAN_REGIONS, parallels, THERMAL_BINS), jnp.float32),
@@ -541,8 +544,9 @@
             jax.ShapeDtypeStruct((OCEAN_REGIONS, parallels), jnp.float32),
             jax.ShapeDtypeStruct((OCEAN_REGIONS, parallels), jnp.float32),
         ),
+        compiler_params=pltpu.CompilerParams(vmem_limit_bytes=SMALL_KERNEL),
         name="finish",
-    )(where_to, shares)
+    )(shares)
     return class_out, jnp.transpose(stream, (0, 2, 1)), heat, implied
 
 

time: 58.3 us -> 52.8 us (0.906)
  local copies, waits for them, and re-layouts: 2.73 us -> 0.04 us
  Pallas kernels: 18.3 us -> 16.2 us
  other arithmetic: 1.53 us -> 0.11 us
  waiting for transfers between devices: 5.26 us -> 6.57 us
  between operations: 1.43 us -> 0.75 us
    slice x2 -> x0, local copies, waits for them, and re-layouts: 1.43 us -> none  [the longest x1 0.92 us: body(): theta_field[:, 0, :]]
    all_to_all x1, waiting for transfers between devices: 5.25 us -> 6.56 us  [exchanged(): return lax.all_to_all(pieces, axis, split_axis=0, concat_axis=0, tiled=True)]
    pallas_call x1, Pallas kernels: 2.49 us -> 1.38 us  [body(): pl.pallas_call(functools.partial(last_kernel, lon_size, lat_size), in_spe...]
    pallas_call x1, Pallas kernels: 2.08 us -> 1.12 us  [body(): pl.pallas_call(functools.partial(finish_kernel, unit_scale, implied_scale...]
    concatenate x2 -> x0, other arithmetic: 0.8 us -> none  [the longest x1 0.73 us: body(): share = jnp.concatenate([share[:SHARE - 1], of_block])]
    convert_element_type x1 -> x0, other arithmetic: 0.7 us -> none  [body(): ocean_tier_tally[0][None].astype(jnp.float32)]
    unnamed x7 -> x6, local copies, waits for them, and re-layouts: 0.61 us -> 0.02 us
    another operation x1 -> x0, local copies, waits for them, and re-layouts: 0.59 us -> none  [body(): jnp.stack([first, (first + 1) % lon_size, start % width, (lat_index == la...]
  transfers between devices with their start and end apart: 3 -> 3, of which waited for: 1 -> 1; matrix products, arithmetic and copies ran while one was open for 5% -> 0% of each run, Pallas kernels for 4% -> 3%
where the time goes in v4:
time: 52.8 us; the launch traced here: 52.5 us
  blocking collectives  19 us (36%)
  Pallas kernels  16.2 us (31%)
  starting transfers between devices  9.89 us (19%)
  waiting for transfers between devices  6.57 us (12%)
  between operations  0.75 us (1%)
    all_to_all x1, blocking collectives, exchanged(): return lax.all_to_all(pieces, axis, split_axis=0, concat_axis=0, tiled=True)  19 us
    pallas_call x1, Pallas kernels, body(): pl.pallas_call(rows_kernel, in_specs=[anywhere, anywhere, in_smem] + [any...  13.7 us
    all_to_all x1, starting transfers between devices, exchanged(): return lax.all_to_all(pieces, axis, split_axis=0, concat_axis=0, tiled=True)  7.18 us
    all_to_all x1, waiting for transfers between devices, exchanged(): return lax.all_to_all(pieces, axis, split_axis=0, concat_axis=0, tiled=True)  6.56 us
    ppermute x1, starting transfers between devices, body(): lax.ppermute(southernmost, 'lat', [(i + 1, i) for i in range(lat_size - 1)])  1.92 us
    pallas_call x1, Pallas kernels, body(): pl.pallas_call(functools.partial(last_kernel, lon_size, lat_size), in_spe...  1.38 us
    pallas_call x1, Pallas kernels, body(): pl.pallas_call(functools.partial(finish_kernel, unit_scale, implied_scale...  1.12 us
  transfers between devices with their start and end apart: 3, of which 1 were waited for; matrix products, arithmetic and copies ran while one was open for 0% of the time, Pallas kernels for 3%

profile of v4, /device:TPU:32, one launch (start us, length us, event | category | flops | bytes accessed | tf_op | source)
XLA Modules:
  0.0 52.5 jit_solution(17493905361415358692)
XLA Ops:
  0.6 13.7 %rows.1 = (f32[16,32,128]{2,1,0:T(8,128)}, f32[56,256]{1,0:T(8,128)}, f32[24,256]{1,0:T(8,128)}) custom-call(f32[16,64,256]{2,1,0:T(8,128)} %theta_hbm.1, f32[16,64,256]{2,1,0:T(8,128)} %speed_hbm.1, f32[16]{0:T(128)} %tier.1, f32[64,256]{1,0:T(8,128)} %zonal_hbm.1, f32[64,256]{1,0:T(8,128)} %plan_hbm.1, f32[64,256]{1,0:T(8,128)} %energy_hbm.1, ...), custom_call_target="tpu_custom_call" | custom-call | flops 8000000000 | bytes 4000000 | tf_op jit(solution)/shard_map/rows/pallas_call | solution.py:475
  14.3 0.0 copy-start.2
  14.3 0.0 copy-start.1
  14.3 7.2 %all-to-all-start = ((f32[16,32,128]{2,1,0:T(8,128)}), f32[16,32,128]{2,1,0:T(8,128)S(1)}, u32[]{:S(2)}, u32[]{:S(2)}) async-start(f32[16,32,128]{2,1,0:T(8,128)} %get-tuple-element.11), calls=%async_computation | async-start | bytes 524288 | tf_op jit(solution)/shard_map/all_to_all | solution.py:445
  21.5 0.0 copy-done.2
  21.5 1.9 %collective-permute-start.1 = (f32[24,256]{1,0:T(8,128)S(1)}, f32[24,256]{1,0:T(8,128)S(1)}, u32[]{:S(2)}, u32[]{:S(2)}) collective-permute-start(f32[24,256]{1,0:T(8,128)S(1)} %copy-done.2), channel_id=1, source_target_pairs={{1,0},{2,1},{3,2},{4,3},{5,4},{6,5},{7,6},{8,7},{9,8},{10,9},{11,1... | collective-permute-start | bytes 73736 | tf_op jit(solution)/shard_map/ppermute | solution.py:512
  23.5 6.6 %all-to-all-done.parcels = f32[16,32,128]{2,1,0:T(8,128)S(1)} async-done(((f32[16,32,128]{2,1,0:T(8,128)}), f32[16,32,128]{2,1,0:T(8,128)S(1)}, u32[]{:S(2)}, u32[]{:S(2)}) %all-to-all-start) | async-done | bytes 262176 | tf_op jit(solution)/shard_map/all_to_all | solution.py:445
  30.1 0.0 copy-start
  30.1 0.8 %collective-permute-start = (f32[1,128]{1,0:T(1,128)S(1)}, f32[1,128]{1,0:T(1,128)S(1)}, u32[]{:S(2)}, u32[]{:S(2)}) collective-permute-start(f32[1,128]{1,0:T(1,128)S(1)} %bitcast.4), channel_id=1, source_target_pairs={{16,17},{17,18},{18,19},{19,20},{20,21},{21,22},{22,23},{23,24},{2... | collective-permute-start | bytes 1544 | tf_op jit(solution)/shard_map/ppermute | solution.py:519
  30.9 0.0 collective-permute-done.1.halo
  30.9 0.0 copy-done.1
  30.9 0.0 copy-done
  30.9 1.4 %last_row.1 = f32[32,128]{1,0:T(8,128)S(1)} custom-call(s32[256]{0:T(256)S(1)} %copy-done, f32[16,32,128]{2,1,0:T(8,128)S(1)} %all-to-all-done.parcels, f32[56,256]{1,0:T(8,128)S(1)} %copy-done.1, f32[24,256]{1,0:T(8,128)S(1)} %collective-permute-done.1.halo), custom_call_target="tpu_custom_call" | custom-call | flops 1000000000 | bytes 600000 | tf_op jit(solution)/shard_map/last_row/pallas_call | solution.py:520
  32.3 0.0 collective-permute-done
  32.3 0.1 broadcast_select_fusion
  32.4 19.0 %all_to_all.10.shares = f32[16,32,128]{2,1,0:T(8,128)S(1)} all-to-all(f32[16,32,128]{2,1,0:T(8,128)S(1)} %broadcast_in_dim.19), channel_id=1, replica_groups=mesh['lon'=16,'lat'=16] {'lon'}, dimensions={0} | all-to-all | bytes 524288 | tf_op jit(solution)/shard_map/all_to_all | solution.py:445
  51.4 1.1 %finish.1 = (f32[4,64,128]{2,1,0:T(8,128)}, f32[4,16,64]{2,1,0:T(8,128)}, f32[4,64]{1,0:T(4,128)}, f32[4,64]{1,0:T(4,128)}) custom-call(f32[16,32,128]{2,1,0:T(8,128)S(1)} %all_to_all.10.shares), custom_call_target="tpu_custom_call" | custom-call | tf_op jit(solution)/shard_map/finish/pallas_call | solution.py:537
  (3 shorter events, 0.1 us)
Async XLA Ops:
  14.3 7.2 %copy-start.2 = (f32[24,256]{1,0:T(8,128)S(1)}, f32[24,256]{1,0:T(8,128)}, u32[]{:S(2)}) copy-start(f32[24,256]{1,0:T(8,128)} %get-tuple-element.13) | copy-start | bytes 73732
  14.3 16.6 %copy-start.1 = (f32[56,256]{1,0:T(8,128)S(1)}, f32[56,256]{1,0:T(8,128)}, u32[]{:S(2)}) copy-start(f32[56,256]{1,0:T(8,128)} %get-tuple-element.12.last) | copy-start | bytes 172036
  14.3 15.7 %all-to-all-start = ((f32[16,32,128]{2,1,0:T(8,128)}), f32[16,32,128]{2,1,0:T(8,128)S(1)}, u32[]{:S(2)}, u32[]{:S(2)}) async-start(f32[16,32,128]{2,1,0:T(8,128)} %get-tuple-element.11), calls=%async_computation | async-start | bytes 524288 | tf_op jit(solution)/shard_map/all_to_all | solution.py:445
  21.5 9.3 %collective-permute-start.1 = (f32[24,256]{1,0:T(8,128)S(1)}, f32[24,256]{1,0:T(8,128)S(1)}, u32[]{:S(2)}, u32[]{:S(2)}) collective-permute-start(f32[24,256]{1,0:T(8,128)S(1)} %copy-done.2), channel_id=1, source_target_pairs={{1,0},{2,1},{3,2},{4,3},{5,4},{6,5},{7,6},{8,7},{9,8},{10,9},{11,1... | collective-permute-start | bytes 73736 | tf_op jit(solution)/shard_map/ppermute | solution.py:512
  30.1 0.8 %copy-start = (s32[256]{0:T(256)S(1)}, s32[256]{0:T(256)}, u32[]{:S(2)}) copy-start(s32[256]{0:T(256)} %seam.1) | copy-start | bytes 3076
  30.1 2.2 %collective-permute-start = (f32[1,128]{1,0:T(1,128)S(1)}, f32[1,128]{1,0:T(1,128)S(1)}, u32[]{:S(2)}, u32[]{:S(2)}) collective-permute-start(f32[1,128]{1,0:T(1,128)S(1)} %bitcast.4), channel_id=1, source_target_pairs={{16,17},{17,18},{18,19},{19,20},{20,21},{21,22},{22,23},{23,24},{2... | collective-permute-start | bytes 1544 | tf_op jit(solution)/shard_map/ppermute | solution.py:519

commit v5 on v4

--- a/solution.py
+++ b/solution.py
@@ -20,11 +20,11 @@
 GROUPS = OCEAN_REGIONS * HIGH
 LANES = 128
 EDGE = 24
-TERMS, TOTALS, LEVEL, PARCEL = 16, 20, 24, 32
-BASIN_UNIT = 32.0
-LAST, LAST_TERMS, SHARE = 20, 24, 32
+TERMS, TOTALS, LEVEL, PARCEL = 16, 20, 22, 32
+LAST, SHARE = 20, 24
+EXTRA = 96
 SMALL_KERNEL = 8 * 1024 * 1024
-LAST_THETA, LAST_VOLUME, LAST_SPEED, LAST_MARKS, LAST_ROWS = 0, 16, 32, 48, 56
+LAST_THETA, LAST_VOLUME, LAST_SPEED, LAST_DEPTH, LAST_BASIN, LAST_ROWS = 0, 16, 32, 48, 49, 56
 HEAT, FLUX, MEAN, WET = 64, 68, 76, 77
 
 
@@ -86,12 +86,32 @@
                     axis=0,
                 )
             )
+        return values, groups
+
+    def alone(self, spread, levels):
+        values, groups = self.row(spread, levels)
         return lax.dot_general(
             jnp.concatenate(values, axis=1),
             jnp.concatenate(groups, axis=1),
             (((1,), (1,)), ((), ())),
             preferred_element_type=jnp.float32,
         )
+
+    def pair(self, spreads, levels):
+        rows = [self.row(spread, levels) for spread in spreads]
+        left = [g if n % 2 else v for n, (v, g) in enumerate(rows)]
+        right = [v if n % 2 else g for n, (v, g) in enumerate(rows)]
+        join = lambda sides: jnp.concatenate(
+            [jnp.concatenate([side[k] for side in sides], axis=0) for k in range(levels)], axis=1
+        )
+        out = lax.dot_general(
+            join(left), join(right), (((1,), (1,)), ((), ())), preferred_element_type=jnp.float32
+        )
+        sums = []
+        for n in range(0, len(rows), 2):
+            o = 96 * (n // 2)
+            sums += [out[o : o + 32, o : o + 64], jnp.transpose(out[o + 32 : o + 96, o + 64 : o + 96])]
+        return sums
 
 
 def class_tile(first, second):
@@ -218,12 +238,13 @@
 
     def rows_of(parts, block, fill):
         sums = []
-        for r in range(ROWS):
-            spread = lambda q, k, count: jnp.broadcast_to(
-                parts[q, k, r : r + 1, :], (count, width)
-            )
-            sums.append(products.row(spread, levels))
-            for k in range(r * levels // ROWS, (r + 1) * levels // ROWS):
+        for start in range(0, ROWS, 2):
+            spreads = [
+                lambda q, k, count, r=r: jnp.broadcast_to(parts[q, k, r : r + 1, :], (count, width))
+                for r in range(start, start + 2)
+            ]
+            sums += products.pair(spreads, levels)
+            for k in range(start * levels // ROWS, (start + 2) * levels // ROWS):
                 fill.level(k)
         for pair in range(ROWS // 2):
             parcel[2 * block + pair // 2, 8 * (pair % 2) : 8 * (pair % 2) + 8, :] = class_tile(
@@ -263,17 +284,19 @@
         south[k : k + 1, :] = theta[k, 0:1, :]
     south[levels : levels + 1, :] = depth[0:1, :].astype(jnp.float32)
     south[levels + 1 :, :] = jnp.zeros((EDGE - levels - 1, width), jnp.float32)
-    marks = (depth[final : final + 1, :] + 32 * label[final : final + 1, :]).astype(jnp.float32)
-    last[LAST_MARKS : LAST_MARKS + 1, :] = marks
-    last[LAST_MARKS + 1 :, :] = jnp.zeros((LAST_ROWS - LAST_MARKS - 1, width), jnp.float32)
+    last[LAST_DEPTH : LAST_DEPTH + 1, :] = depth[final : final + 1, :].astype(jnp.float32)
+    last[LAST_BASIN : LAST_BASIN + 1, :] = label[final : final + 1, :].astype(jnp.float32)
+    last[LAST_BASIN + 1 :, :] = jnp.zeros((LAST_ROWS - LAST_BASIN - 1, width), jnp.float32)
     totals = jnp.zeros((ROWS, LANES), jnp.float32)
     for d in range(0, 2 * blocks, 2):
         totals = totals + parcel[d, TERMS : TERMS + 8, :]
-    totals = jnp.sum(totals, axis=0, keepdims=True)
+    totals = pltpu.roll(jnp.sum(totals, axis=0, keepdims=True), LANES // 4, 1)
     for d in range(2 * blocks):
         parcel[d, TOTALS : TOTALS + 1, :] = totals
         parcel[d, TOTALS + 1 : LEVEL, :] = jnp.zeros((LEVEL - TOTALS - 1, LANES), jnp.float32)
-        for n, q in enumerate((LAST_THETA + d, LAST_VOLUME + d, LAST_SPEED + d, LAST_MARKS)):
+        for n, q in enumerate(
+            (LAST_THETA + d, LAST_VOLUME + d, LAST_SPEED + d, LAST_DEPTH, LAST_BASIN)
+        ):
             row = last[q : q + 1, :]
             parcel[d, LEVEL + 2 * n : LEVEL + 2 * n + 1, :] = row[:, :half]
             parcel[d, LEVEL + 2 * n + 1 : LEVEL + 2 * n + 2, :] = row[:, half:]
@@ -315,13 +338,11 @@
 
     high, rest = split_in_two(mirrored(0))
     middle, lowest = split_in_two(rest)
-    blocks_marks = mirrored(3)
-    blocks_depth = blocks_marks - BASIN_UNIT * jnp.floor(blocks_marks * (1.0 / BASIN_UNIT))
     source = lax.broadcasted_iota(jnp.int32, (2 * width, width), 0)
     target = lax.broadcasted_iota(jnp.int32, (2 * width, width), 1)
     mirror = jnp.where(source + target == offset + (width - 1), 1.0, 0.0).astype(jnp.bfloat16)
     pieces = jnp.dot(
-        jnp.concatenate([high, middle, lowest, blocks_depth], axis=0).astype(jnp.bfloat16),
+        jnp.concatenate([high, middle, lowest, mirrored(3)], axis=0).astype(jnp.bfloat16),
         mirror,
         preferred_element_type=jnp.float32,
     )
@@ -331,19 +352,19 @@
     theta = jnp.where(at_fold, whole_row(0), last[LAST_THETA : LAST_THETA + levels, :])
     full_volume = jnp.where(at_fold, whole_row(1), last[LAST_VOLUME : LAST_VOLUME + levels, :])
     speed = jnp.where(at_fold, whole_row(2), last[LAST_SPEED : LAST_SPEED + levels, :])
-    marks = jnp.where(at_fold, whole_row(3), spread_out(last[LAST_MARKS : LAST_MARKS + 1, :]))
+    depth = jnp.where(at_fold, whole_row(3), spread_out(last[LAST_DEPTH : LAST_DEPTH + 1, :]))
+    basin = jnp.where(at_fold, whole_row(4), spread_out(last[LAST_BASIN : LAST_BASIN + 1, :]))
     north = jnp.where(at_fold, folded, halo[0:levels, :])
     north_depth = jnp.where(at_fold, pieces[48:64], spread_out(halo[levels : levels + 1, :]))
-    basin = jnp.floor(marks * (1.0 / BASIN_UNIT))
     face = 0.5 * (theta + north)
-    face_depth = jnp.minimum(marks - BASIN_UNIT * basin, north_depth)
+    face_depth = jnp.minimum(depth, north_depth)
     row_id = lax.broadcasted_iota(jnp.int32, (levels, width), 0)
     level_id = jnp.where(at_fold, lon_index, row_id).astype(jnp.float32)
     volume = jnp.where(level_id < face_depth, full_volume, 0.0)
     transport = volume * speed
     for q, value in enumerate(interpolation(face, transport, basin * float(HIGH))):
         parts[q] = value
-    sums = Products(width).row(
+    sums = Products(width).alone(
         lambda q, k, count: jnp.broadcast_to(parts[q, k : k + 1, :], (count, width)), levels
     )
     last_class = class_tile(sums, jnp.zeros_like(sums))
@@ -397,43 +418,46 @@
     )
     placed = placed[0:EDGE] + placed[EDGE : 2 * EDGE]
     share[0:16, :] = placed[0:16]
-    share[TERMS : TERMS + 4, :] = total[TERMS : TERMS + 4]
+    for n in range(4):
+        own = pltpu.roll(terms, EXTRA - n * (LANES // 4), 1)
+        share[TERMS + n : TERMS + n + 1, :] = jnp.where(
+            lane1 >= EXTRA, own, total[TERMS + n : TERMS + n + 1]
+        )
     share[LAST : LAST + 4, :] = placed[16:20]
-    share[LAST_TERMS : LAST_TERMS + 1, :] = terms
-    share[LAST_TERMS + 1 :, :] = jnp.zeros((SHARE - LAST_TERMS - 1, LANES), jnp.float32)
 
 
 def finish_kernel(unit_scale, implied_scale, shares, class_out, stream, heat, implied):
     devices = shares.shape[0]
     rows = 4 * devices
     levels = stream.shape[1]
-    mine = shares[0, LAST:SHARE, :]
+    mine = shares[0, TERMS:SHARE, :]
     for d in range(1, devices):
-        mine = mine + shares[d, LAST:SHARE, :]
+        mine = mine + shares[d, TERMS:SHARE, :]
+    lane = lax.broadcasted_iota(jnp.int32, (1, LANES), 1)
+    own_terms = jnp.zeros((1, LANES), jnp.float32)
+    for n in range(3):
+        quarter = pltpu.roll(mine[n : n + 1], (n + 1) * (LANES // 4), 1)
+        own_terms = jnp.where(lane // (LANES // 4) == n, quarter, own_terms)
+    offsets = mine[3:4]
     for b in range(OCEAN_REGIONS):
         for d in range(devices):
             class_out[b, 4 * d : 4 * d + 4, :] = unit_scale * shares[d, 4 * b : 4 * b + 4, :]
-        class_out[b, rows - 1 : rows, :] += unit_scale * mine[b : b + 1]
+        class_out[b, rows - 1 : rows, :] += unit_scale * mine[LAST - TERMS + b : LAST - TERMS + b + 1]
     terms = jnp.concatenate([shares[d, TERMS : TERMS + 4, :] for d in range(devices)], axis=0)
     row_id = lax.broadcasted_iota(jnp.int32, terms.shape, 0)
-    own_terms = mine[LAST_TERMS - LAST : LAST_TERMS - LAST + 1]
     terms = terms + jnp.where(row_id == rows - 1, jnp.broadcast_to(own_terms, terms.shape), 0.0)
     turned = jnp.transpose(
         jnp.concatenate([terms, jnp.zeros((LANES - rows, LANES), jnp.float32)], axis=0)
     )
     for b in range(OCEAN_REGIONS):
         stream[b] = unit_scale * turned[b * levels : (b + 1) * levels, :rows]
-    lane = lax.broadcasted_iota(jnp.int32, (1, LANES), 1)
     row_mean = turned[MEAN : MEAN + 1] / jnp.where(lane < rows, turned[WET : WET + 1], 1.0)
-    offsets = jnp.zeros((1, LANES), jnp.float32)
-    for d in range(devices):
-        offsets += shares[d, SHARE - 1 : SHARE, :]
     for b in range(OCEAN_REGIONS):
         total = turned[(b + 1) * levels - 1 : (b + 1) * levels]
         out = unit_scale / 16.0 * (turned[HEAT + b : HEAT + b + 1] - total * row_mean)
         heat[b : b + 1, :] = out[:, :rows]
         flux = turned[FLUX + b : FLUX + b + 1]
-        offset = over_longitude(jnp.where(lane == FLUX + b, offsets, 0.0))
+        offset = over_longitude(jnp.where(lane == FLUX + LANES // 4 + b, offsets, 0.0))
         shift = 1
         while shift < rows:
             flux = flux + jnp.where(lane >= shift, pltpu.roll(flux, shift, 1), 0.0)
@@ -532,7 +556,8 @@
         name="last_row",
     )(seam_matching_meridian, received, last, halo)
     row_id = lax.broadcasted_iota(jnp.int32, share.shape, 0)
-    share = jnp.where(row_id == SHARE - 1, of_block, share)
+    lane = lax.broadcasted_iota(jnp.int32, share.shape, 1)
+    share = jnp.where((row_id == TERMS + 3) & (lane >= EXTRA), of_block, share)
     shares = exchanged(jnp.broadcast_to(share, (lon_size, SHARE, LANES)), "lon")
     class_out, stream, heat, implied = pl.pallas_call(
         functools.partial(finish_kernel, unit_scale, implied_scale),

time: 52.8 us -> 51.8 us (0.981)
  Pallas kernels: 16.2 us -> 15.5 us
    pallas_call x1, Pallas kernels: 13.7 us -> 13 us  [body(): pl.pallas_call(rows_kernel, in_specs=[anywhere, anywhere, in_smem] + [any...]
where the time goes in v5:
time: 51.8 us; the launch traced here: 51.5 us
  blocking collectives  18.6 us (36%)
  Pallas kernels  15.5 us (30%)
  starting transfers between devices  9.9 us (19%)
  waiting for transfers between devices  6.56 us (13%)
  between operations  0.75 us (1%)
    all_to_all x1, blocking collectives, exchanged(): return lax.all_to_all(pieces, axis, split_axis=0, concat_axis=0, tiled=True)  18.6 us
    pallas_call x1, Pallas kernels, body(): pl.pallas_call(rows_kernel, in_specs=[anywhere, anywhere, in_smem] + [any...  13 us
    all_to_all x1, starting transfers between devices, exchanged(): return lax.all_to_all(pieces, axis, split_axis=0, concat_axis=0, tiled=True)  7.18 us
    all_to_all x1, waiting for transfers between devices, exchanged(): return lax.all_to_all(pieces, axis, split_axis=0, concat_axis=0, tiled=True)  6.55 us
    ppermute x1, starting transfers between devices, body(): lax.ppermute(southernmost, 'lat', [(i + 1, i) for i in range(lat_size - 1)])  1.92 us
    pallas_call x1, Pallas kernels, body(): pl.pallas_call(functools.partial(last_kernel, lon_size, lat_size), in_spe...  1.38 us
    pallas_call x1, Pallas kernels, body(): pl.pallas_call(functools.partial(finish_kernel, unit_scale, implied_scale...  1.2 us
  transfers between devices with their start and end apart: 3, of which 1 were waited for; matrix products, arithmetic and copies ran while one was open for 0% of the time, Pallas kernels for 3%

profile of v5, /device:TPU:32, one launch (start us, length us, event | category | flops | bytes accessed | tf_op | source)
XLA Modules:
  0.0 51.5 jit_solution(13172921852829277630)
XLA Ops:
  0.6 13.0 %rows.1 = (f32[16,32,128]{2,1,0:T(8,128)}, f32[56,256]{1,0:T(8,128)}, f32[24,256]{1,0:T(8,128)}) custom-call(f32[16,64,256]{2,1,0:T(8,128)} %theta_hbm.1, f32[16,64,256]{2,1,0:T(8,128)} %speed_hbm.1, f32[16]{0:T(128)} %tier.1, f32[64,256]{1,0:T(8,128)} %zonal_hbm.1, f32[64,256]{1,0:T(8,128)} %plan_hbm.1, f32[64,256]{1,0:T(8,128)} %energy_hbm.1, ...), custom_call_target="tpu_custom_call" | custom-call | flops 8000000000 | bytes 4000000 | tf_op jit(solution)/shard_map/rows/pallas_call | solution.py:499
  13.6 0.0 copy-start.2
  13.6 0.0 copy-start.1
  13.6 7.2 %all-to-all-start = ((f32[16,32,128]{2,1,0:T(8,128)}), f32[16,32,128]{2,1,0:T(8,128)S(1)}, u32[]{:S(2)}, u32[]{:S(2)}) async-start(f32[16,32,128]{2,1,0:T(8,128)} %get-tuple-element.11), calls=%async_computation | async-start | bytes 524288 | tf_op jit(solution)/shard_map/all_to_all | solution.py:469
  20.8 0.0 copy-done.2
  20.8 1.9 %collective-permute-start.1 = (f32[24,256]{1,0:T(8,128)S(1)}, f32[24,256]{1,0:T(8,128)S(1)}, u32[]{:S(2)}, u32[]{:S(2)}) collective-permute-start(f32[24,256]{1,0:T(8,128)S(1)} %copy-done.2), channel_id=1, source_target_pairs={{1,0},{2,1},{3,2},{4,3},{5,4},{6,5},{7,6},{8,7},{9,8},{10,9},{11,1... | collective-permute-start | bytes 73736 | tf_op jit(solution)/shard_map/ppermute | solution.py:536
  22.8 6.6 %all-to-all-done.parcels = f32[16,32,128]{2,1,0:T(8,128)S(1)} async-done(((f32[16,32,128]{2,1,0:T(8,128)}), f32[16,32,128]{2,1,0:T(8,128)S(1)}, u32[]{:S(2)}, u32[]{:S(2)}) %all-to-all-start) | async-done | bytes 262176 | tf_op jit(solution)/shard_map/all_to_all | solution.py:469
  29.4 0.0 copy-start
  29.4 0.8 %collective-permute-start = (f32[1,128]{1,0:T(1,128)S(1)}, f32[1,128]{1,0:T(1,128)S(1)}, u32[]{:S(2)}, u32[]{:S(2)}) collective-permute-start(f32[1,128]{1,0:T(1,128)S(1)} %bitcast.4), channel_id=1, source_target_pairs={{16,17},{17,18},{18,19},{19,20},{20,21},{21,22},{22,23},{23,24},{2... | collective-permute-start | bytes 1544 | tf_op jit(solution)/shard_map/ppermute | solution.py:543
  30.2 0.0 collective-permute-done.1.halo
  30.2 0.0 copy-done.1
  30.2 0.0 copy-done
  30.2 1.4 %last_row.1 = f32[24,128]{1,0:T(8,128)S(1)} custom-call(s32[256]{0:T(256)S(1)} %copy-done, f32[16,32,128]{2,1,0:T(8,128)S(1)} %all-to-all-done.parcels, f32[56,256]{1,0:T(8,128)S(1)} %copy-done.1, f32[24,256]{1,0:T(8,128)S(1)} %collective-permute-done.1.halo), custom_call_target="tpu_custom_call" | custom-call | flops 1000000000 | bytes 600000 | tf_op jit(solution)/shard_map/last_row/pallas_call | solution.py:544
  31.6 0.0 collective-permute-done
  31.6 0.1 and_select_fusion
  31.7 18.6 %all_to_all.10.shares = f32[16,24,128]{2,1,0:T(8,128)S(1)} all-to-all(f32[16,24,128]{2,1,0:T(8,128)S(1)} %broadcast_in_dim.19), channel_id=1, replica_groups=mesh['lon'=16,'lat'=16] {'lon'}, dimensions={0} | all-to-all | bytes 393216 | tf_op jit(solution)/shard_map/all_to_all | solution.py:469
  50.3 1.2 %finish.1 = (f32[4,64,128]{2,1,0:T(8,128)}, f32[4,16,64]{2,1,0:T(8,128)}, f32[4,64]{1,0:T(4,128)}, f32[4,64]{1,0:T(4,128)}) custom-call(f32[16,24,128]{2,1,0:T(8,128)S(1)} %all_to_all.10.shares), custom_call_target="tpu_custom_call" | custom-call | tf_op jit(solution)/shard_map/finish/pallas_call | solution.py:562
  (4 shorter events, 0.1 us)
Async XLA Ops:
  13.6 7.2 %copy-start.2 = (f32[24,256]{1,0:T(8,128)S(1)}, f32[24,256]{1,0:T(8,128)}, u32[]{:S(2)}) copy-start(f32[24,256]{1,0:T(8,128)} %get-tuple-element.13) | copy-start | bytes 73732
  13.6 16.6 %copy-start.1 = (f32[56,256]{1,0:T(8,128)S(1)}, f32[56,256]{1,0:T(8,128)}, u32[]{:S(2)}) copy-start(f32[56,256]{1,0:T(8,128)} %get-tuple-element.12.last) | copy-start | bytes 172036
  13.6 15.7 %all-to-all-start = ((f32[16,32,128]{2,1,0:T(8,128)}), f32[16,32,128]{2,1,0:T(8,128)S(1)}, u32[]{:S(2)}, u32[]{:S(2)}) async-start(f32[16,32,128]{2,1,0:T(8,128)} %get-tuple-element.11), calls=%async_computation | async-start | bytes 524288 | tf_op jit(solution)/shard_map/all_to_all | solution.py:469
  20.8 9.3 %collective-permute-start.1 = (f32[24,256]{1,0:T(8,128)S(1)}, f32[24,256]{1,0:T(8,128)S(1)}, u32[]{:S(2)}, u32[]{:S(2)}) collective-permute-start(f32[24,256]{1,0:T(8,128)S(1)} %copy-done.2), channel_id=1, source_target_pairs={{1,0},{2,1},{3,2},{4,3},{5,4},{6,5},{7,6},{8,7},{9,8},{10,9},{11,1... | collective-permute-start | bytes 73736 | tf_op jit(solution)/shard_map/ppermute | solution.py:536
  29.4 0.8 %copy-start = (s32[256]{0:T(256)S(1)}, s32[256]{0:T(256)}, u32[]{:S(2)}) copy-start(s32[256]{0:T(256)} %seam.1) | copy-start | bytes 3076
  29.4 2.2 %collective-permute-start = (f32[1,128]{1,0:T(1,128)S(1)}, f32[1,128]{1,0:T(1,128)S(1)}, u32[]{:S(2)}, u32[]{:S(2)}) collective-permute-start(f32[1,128]{1,0:T(1,128)S(1)} %bitcast.4), channel_id=1, source_target_pairs={{16,17},{17,18},{18,19},{19,20},{20,21},{21,22},{22,23},{23,24},{2... | collective-permute-start | bytes 1544 | tf_op jit(solution)/shard_map/ppermute | solution.py:543

commit v6 on v5

--- a/solution.py
+++ b/solution.py
@@ -37,14 +37,14 @@
     return jnp.sum(x, axis=1, keepdims=True)
 
 
-def interpolation(face, transport, basin_base):
+def interpolation(face, transport):
     per_bin = THERMAL_BINS / THERMAL_RANGE
     position = jnp.clip((face - THERMAL_FLOOR) * per_bin, 0.0, THERMAL_BINS - 1.0)
     low_bin = jnp.minimum(jnp.floor(position), THERMAL_BINS - 2.0)
     digit = jnp.floor(low_bin * (1.0 / LOW))
     weighted = transport * (position - low_bin)
     return (
-        basin_base + digit,
+        digit,
         low_bin - LOW * digit,
         *split_in_two(transport),
         *split_in_two(weighted),
@@ -55,21 +55,22 @@
     def __init__(self, width):
         packed_id = lax.broadcasted_iota(jnp.int32, (16, width), 0)
         as_packed = lambda x: x.astype(jnp.float32).astype(jnp.bfloat16)
-        self.group_ids = [as_packed(packed_id + 16 * t) for t in range(GROUPS // 16)]
+        self.high_ids = as_packed(packed_id)
         self.low_ids = as_packed(packed_id & (LOW - 1))
         self.one = jnp.ones((16, width), jnp.bfloat16)
         self.none = jnp.zeros((16, width), jnp.bfloat16)
         self.width = width
 
-    def row(self, spread, levels):
+    def indicators(self, basin):
+        basin = basin.astype(jnp.bfloat16)
+        return [jnp.where(basin == b, self.one, self.none) for b in range(OCEAN_REGIONS)]
+
+    def row(self, spread, in_basin, levels):
         values, groups = [], []
         for k in range(levels):
-            group = spread(0, k, 16).astype(jnp.bfloat16)
-            groups.append(
-                jnp.concatenate(
-                    [jnp.where(group == g, self.one, self.none) for g in self.group_ids], axis=0
-                )
-            )
+            at_high = spread(0, k, 16).astype(jnp.bfloat16) == self.high_ids
+            at_high = jnp.where(at_high, self.one, self.none)
+            groups.append(jnp.concatenate([at_high * x for x in in_basin(k)], axis=0))
             at_low = spread(1, k, 16).astype(jnp.bfloat16) == self.low_ids
             values.append(
                 jnp.concatenate(
@@ -88,8 +89,8 @@
             )
         return values, groups
 
-    def alone(self, spread, levels):
-        values, groups = self.row(spread, levels)
+    def alone(self, spread, in_basin, levels):
+        values, groups = self.row(spread, in_basin, levels)
         return lax.dot_general(
             jnp.concatenate(values, axis=1),
             jnp.concatenate(groups, axis=1),
@@ -97,8 +98,11 @@
             preferred_element_type=jnp.float32,
         )
 
-    def pair(self, spreads, levels):
-        rows = [self.row(spread, levels) for spread in spreads]
+    def pair(self, spreads, basins, levels):
+        rows = []
+        for spread, basin in zip(spreads, basins):
+            here = self.indicators(basin)
+            rows.append(self.row(spread, lambda k, here=here: here, levels))
         left = [g if n % 2 else v for n, (v, g) in enumerate(rows)]
         right = [v if n % 2 else g for n, (v, g) in enumerate(rows)]
         join = lambda sides: jnp.concatenate(
@@ -145,6 +149,8 @@
     label,
     even,
     odd,
+    even_basins,
+    odd_basins,
     field_sems,
     plane_sems,
 ):
@@ -171,10 +177,12 @@
             )
         )
     ]
+    for copy in planes[:3]:
+        copy.start()
     field_copy(0, 0).start()
-    for copy in planes:
+    field_copy(1, 0).start()
+    for copy in planes[3:]:
         copy.start()
-    field_copy(1, 0).start()
     for c in range(1, chunks):
         field_copy(0, c).start()
         field_copy(1, c).start()
@@ -187,7 +195,7 @@
         return jnp.where(last_row, jnp.broadcast_to(beyond, own.shape), pltpu.roll(own, ROWS - 1, 0))
 
     class Block:
-        def __init__(self, block, parts):
+        def __init__(self, block, parts, basins):
             self.block, self.parts = block, parts
             self.rows = pl.ds(pl.multiple_of(block * ROWS, ROWS), ROWS)
             ahead = jnp.minimum(block + 1, blocks - 1) * ROWS
@@ -197,10 +205,9 @@
             next_depth = jnp.where(block == blocks - 1, 0.0, next_depth)
             self.face_depth = jnp.minimum(own_depth, northern(own_depth, next_depth))
             basin = label[self.rows, :]
-            self.basin_base = basin.astype(jnp.float32) * float(HIGH)
+            basins[...] = basin.astype(jnp.float32)
             self.in_basin = [basin == b for b in range(OCEAN_REGIONS)]
             self.span = zonal[self.rows, :]
-            self.flux = energy[self.rows, :] * plan[self.rows, :]
             self.terms = jnp.zeros((ROWS, LANES), jnp.float32)
             self.running = [jnp.zeros((ROWS, 1), jnp.float32) for _ in range(OCEAN_REGIONS)]
             self.mean_sum = jnp.zeros((ROWS, width), jnp.float32)
@@ -212,7 +219,7 @@
             face = 0.5 * (own + northern(own, theta[k, self.beyond, :][0:1]))
             volume = jnp.where(self.face_depth > float(k), tier[k] * self.span, 0.0)
             transport = volume * speed[k, self.rows, :]
-            for q, value in enumerate(interpolation(face, transport, self.basin_base)):
+            for q, value in enumerate(interpolation(face, transport)):
                 self.parts[q, k] = value
             self.mean_sum += volume * face
             self.wet_sum += volume
@@ -223,11 +230,12 @@
 
         def close(self):
             terms = self.terms
+            total_flux = energy[self.rows, :] * plan[self.rows, :]
             for b in range(OCEAN_REGIONS):
                 here = self.in_basin[b]
                 heat = over_longitude(jnp.where(here, self.heat_sum, 0.0))
                 terms = jnp.where(lane == HEAT + b, heat, terms)
-                flux = over_longitude(jnp.where(here, self.flux, 0.0))
+                flux = over_longitude(jnp.where(here, total_flux, 0.0))
                 terms = jnp.where(lane == FLUX + b, flux, terms)
             terms = jnp.where(lane == MEAN, over_longitude(self.mean_sum), terms)
             terms = jnp.where(lane == WET, over_longitude(self.wet_sum), terms)
@@ -236,29 +244,32 @@
 
     products = Products(width)
 
-    def rows_of(parts, block, fill):
-        sums = []
-        for start in range(0, ROWS, 2):
+    def rows_of(parts, basins, block, fill):
+        for pair in range(ROWS // 2):
+            first = 2 * pair
+            for k in range(first * levels // ROWS, (first + 2) * levels // ROWS):
+                fill.level(k)
             spreads = [
                 lambda q, k, count, r=r: jnp.broadcast_to(parts[q, k, r : r + 1, :], (count, width))
-                for r in range(start, start + 2)
+                for r in (first, first + 1)
             ]
-            sums += products.pair(spreads, levels)
-            for k in range(start * levels // ROWS, (start + 2) * levels // ROWS):
-                fill.level(k)
-        for pair in range(ROWS // 2):
-            parcel[2 * block + pair // 2, 8 * (pair % 2) : 8 * (pair % 2) + 8, :] = class_tile(
-                sums[2 * pair], sums[2 * pair + 1]
-            )
+            labels = [
+                jnp.broadcast_to(basins[r : r + 1, :], (16, width)) for r in (first, first + 1)
+            ]
+            sums = products.pair(spreads, labels, levels)
+            tile = class_tile(*sums)
+            parcel[2 * block + pair // 2, 8 * (pair % 2) : 8 * (pair % 2) + 8, :] = tile
         fill.close()
 
-    for copy in planes:
+    for copy in planes[:3]:
         copy.wait()
     field_copy(0, 0).wait()
     field_copy(1, 0).wait()
-    opening = Block(jnp.int32(0), even)
+    opening = Block(jnp.int32(0), even, even_basins)
     for k in range(levels):
         opening.level(k)
+    for copy in planes[3:]:
+        copy.wait()
     opening.close()
 
     def two_blocks(i, carry):
@@ -267,8 +278,9 @@
             field_copy(0, i + 1).wait()
             field_copy(1, i + 1).wait()
 
-        rows_of(even, 2 * i, Block(2 * i + 1, odd))
-        rows_of(odd, 2 * i + 1, Block(jnp.minimum(2 * i + 2, blocks - 1), even))
+        rows_of(even, even_basins, 2 * i, Block(2 * i + 1, odd, odd_basins))
+        ahead = jnp.minimum(2 * i + 2, blocks - 1)
+        rows_of(odd, odd_basins, 2 * i + 1, Block(ahead, even, even_basins))
         return carry
 
     lax.fori_loop(0, chunks, two_blocks, 0)
@@ -362,11 +374,12 @@
     level_id = jnp.where(at_fold, lon_index, row_id).astype(jnp.float32)
     volume = jnp.where(level_id < face_depth, full_volume, 0.0)
     transport = volume * speed
-    for q, value in enumerate(interpolation(face, transport, basin * float(HIGH))):
+    for q, value in enumerate(interpolation(face, transport)):
         parts[q] = value
-    sums = Products(width).alone(
-        lambda q, k, count: jnp.broadcast_to(parts[q, k : k + 1, :], (count, width)), levels
-    )
+    parts[6] = basin
+    products = Products(width)
+    spread = lambda q, k, count: jnp.broadcast_to(parts[q, k : k + 1, :], (count, width))
+    sums = products.alone(spread, lambda k: products.indicators(spread(6, k, 16)), levels)
     last_class = class_tile(sums, jnp.zeros_like(sums))
 
     lane = lax.broadcasted_iota(jnp.int32, (levels, LANES), 1)
@@ -515,6 +528,8 @@
             plane_i32,
             parts,
             parts,
+            pltpu.VMEM((ROWS, width), jnp.float32),
+            pltpu.VMEM((ROWS, width), jnp.float32),
             pltpu.SemaphoreType.DMA((2, chunks)),
             pltpu.SemaphoreType.DMA((5,)),
         ],
@@ -547,7 +562,7 @@
         out_specs=in_vmem,
         out_shape=jax.ShapeDtypeStruct((SHARE, LANES), jnp.float32),
         scratch_shapes=[
-            pltpu.VMEM((6, levels, width), jnp.float32),
+            pltpu.VMEM((7, levels, width), jnp.float32),
         ],
         compiler_params=pltpu.CompilerParams(vmem_limit_bytes=SMALL_KERNEL),
         cost_estimate=pl.CostEstimate(

time: 51.8 us -> 51.1 us (0.986)
  Pallas kernels: 15.5 us -> 14.8 us
    pallas_call x1, Pallas kernels: 13 us -> 12.2 us  [body(): pl.pallas_call(rows_kernel, in_specs=[anywhere, anywhere, in_smem] + [any...]
where the time goes in v6:
time: 51.1 us; the launch traced here: 50.8 us
  blocking collectives  18.6 us (36%)
  Pallas kernels  14.8 us (29%)
  starting transfers between devices  9.89 us (19%)
  waiting for transfers between devices  6.56 us (13%)
  between operations  0.75 us (1%)
    all_to_all x1, blocking collectives, exchanged(): return lax.all_to_all(pieces, axis, split_axis=0, concat_axis=0, tiled=True)  18.6 us
    pallas_call x1, Pallas kernels, body(): pl.pallas_call(rows_kernel, in_specs=[anywhere, anywhere, in_smem] + [any...  12.2 us
    all_to_all x1, starting transfers between devices, exchanged(): return lax.all_to_all(pieces, axis, split_axis=0, concat_axis=0, tiled=True)  7.18 us
    all_to_all x1, waiting for transfers between devices, exchanged(): return lax.all_to_all(pieces, axis, split_axis=0, concat_axis=0, tiled=True)  6.55 us
    ppermute x1, starting transfers between devices, body(): lax.ppermute(southernmost, 'lat', [(i + 1, i) for i in range(lat_size - 1)])  1.92 us
    pallas_call x1, Pallas kernels, body(): pl.pallas_call(functools.partial(last_kernel, lon_size, lat_size), in_spe...  1.4 us
    pallas_call x1, Pallas kernels, body(): pl.pallas_call(functools.partial(finish_kernel, unit_scale, implied_scale...  1.2 us
  transfers between devices with their start and end apart: 3, of which 1 were waited for; matrix products, arithmetic and copies ran while one was open for 0% of the time, Pallas kernels for 3%

profile of v6, /device:TPU:32, one launch (start us, length us, event | category | flops | bytes accessed | tf_op | source)
XLA Modules:
  0.0 50.8 jit_solution(15835960173204605122)
XLA Ops:
  0.6 12.2 %rows.1 = (f32[16,32,128]{2,1,0:T(8,128)}, f32[56,256]{1,0:T(8,128)}, f32[24,256]{1,0:T(8,128)}) custom-call(f32[16,64,256]{2,1,0:T(8,128)} %theta_hbm.1, f32[16,64,256]{2,1,0:T(8,128)} %speed_hbm.1, f32[16]{0:T(128)} %tier.1, f32[64,256]{1,0:T(8,128)} %zonal_hbm.1, f32[64,256]{1,0:T(8,128)} %plan_hbm.1, f32[64,256]{1,0:T(8,128)} %energy_hbm.1, ...), custom_call_target="tpu_custom_call" | custom-call | flops 8000000000 | bytes 4000000 | tf_op jit(solution)/shard_map/rows/pallas_call | solution.py:512
  12.9 0.0 copy-start.2
  12.9 0.0 copy-start.1
  12.9 7.2 %all-to-all-start = ((f32[16,32,128]{2,1,0:T(8,128)}), f32[16,32,128]{2,1,0:T(8,128)S(1)}, u32[]{:S(2)}, u32[]{:S(2)}) async-start(f32[16,32,128]{2,1,0:T(8,128)} %get-tuple-element.11), calls=%async_computation | async-start | bytes 524288 | tf_op jit(solution)/shard_map/all_to_all | solution.py:482
  20.1 0.0 copy-done.2
  20.1 1.9 %collective-permute-start.1 = (f32[24,256]{1,0:T(8,128)S(1)}, f32[24,256]{1,0:T(8,128)S(1)}, u32[]{:S(2)}, u32[]{:S(2)}) collective-permute-start(f32[24,256]{1,0:T(8,128)S(1)} %copy-done.2), channel_id=1, source_target_pairs={{1,0},{2,1},{3,2},{4,3},{5,4},{6,5},{7,6},{8,7},{9,8},{10,9},{11,1... | collective-permute-start | bytes 73736 | tf_op jit(solution)/shard_map/ppermute | solution.py:551
  22.1 6.6 %all-to-all-done.parcels = f32[16,32,128]{2,1,0:T(8,128)S(1)} async-done(((f32[16,32,128]{2,1,0:T(8,128)}), f32[16,32,128]{2,1,0:T(8,128)S(1)}, u32[]{:S(2)}, u32[]{:S(2)}) %all-to-all-start) | async-done | bytes 262176 | tf_op jit(solution)/shard_map/all_to_all | solution.py:482
  28.6 0.0 copy-start
  28.6 0.8 %collective-permute-start = (f32[1,128]{1,0:T(1,128)S(1)}, f32[1,128]{1,0:T(1,128)S(1)}, u32[]{:S(2)}, u32[]{:S(2)}) collective-permute-start(f32[1,128]{1,0:T(1,128)S(1)} %bitcast.4), channel_id=1, source_target_pairs={{16,17},{17,18},{18,19},{19,20},{20,21},{21,22},{22,23},{23,24},{2... | collective-permute-start | bytes 1544 | tf_op jit(solution)/shard_map/ppermute | solution.py:558
  29.4 0.0 collective-permute-done.1.halo
  29.5 0.0 copy-done.1
  29.5 0.0 copy-done
  29.5 1.4 %last_row.1 = f32[24,128]{1,0:T(8,128)S(1)} custom-call(s32[256]{0:T(256)S(1)} %copy-done, f32[16,32,128]{2,1,0:T(8,128)S(1)} %all-to-all-done.parcels, f32[56,256]{1,0:T(8,128)S(1)} %copy-done.1, f32[24,256]{1,0:T(8,128)S(1)} %collective-permute-done.1.halo), custom_call_target="tpu_custom_call" | custom-call | flops 1000000000 | bytes 600000 | tf_op jit(solution)/shard_map/last_row/pallas_call | solution.py:559
  30.9 0.0 collective-permute-done
  30.9 0.1 and_select_fusion
  31.0 18.6 %all_to_all.10.shares = f32[16,24,128]{2,1,0:T(8,128)S(1)} all-to-all(f32[16,24,128]{2,1,0:T(8,128)S(1)} %broadcast_in_dim.19), channel_id=1, replica_groups=mesh['lon'=16,'lat'=16] {'lon'}, dimensions={0} | all-to-all | bytes 393216 | tf_op jit(solution)/shard_map/all_to_all | solution.py:482
  49.6 1.2 %finish.1 = (f32[4,64,128]{2,1,0:T(8,128)}, f32[4,16,64]{2,1,0:T(8,128)}, f32[4,64]{1,0:T(4,128)}, f32[4,64]{1,0:T(4,128)}) custom-call(f32[16,24,128]{2,1,0:T(8,128)S(1)} %all_to_all.10.shares), custom_call_target="tpu_custom_call" | custom-call | tf_op jit(solution)/shard_map/finish/pallas_call | solution.py:577
  (4 shorter events, 0.1 us)
Async XLA Ops:
  12.9 7.2 %copy-start.2 = (f32[24,256]{1,0:T(8,128)S(1)}, f32[24,256]{1,0:T(8,128)}, u32[]{:S(2)}) copy-start(f32[24,256]{1,0:T(8,128)} %get-tuple-element.13) | copy-start | bytes 73732
  12.9 16.6 %copy-start.1 = (f32[56,256]{1,0:T(8,128)S(1)}, f32[56,256]{1,0:T(8,128)}, u32[]{:S(2)}) copy-start(f32[56,256]{1,0:T(8,128)} %get-tuple-element.12.last) | copy-start | bytes 172036
  12.9 15.7 %all-to-all-start = ((f32[16,32,128]{2,1,0:T(8,128)}), f32[16,32,128]{2,1,0:T(8,128)S(1)}, u32[]{:S(2)}, u32[]{:S(2)}) async-start(f32[16,32,128]{2,1,0:T(8,128)} %get-tuple-element.11), calls=%async_computation | async-start | bytes 524288 | tf_op jit(solution)/shard_map/all_to_all | solution.py:482
  20.1 9.3 %collective-permute-start.1 = (f32[24,256]{1,0:T(8,128)S(1)}, f32[24,256]{1,0:T(8,128)S(1)}, u32[]{:S(2)}, u32[]{:S(2)}) collective-permute-start(f32[24,256]{1,0:T(8,128)S(1)} %copy-done.2), channel_id=1, source_target_pairs={{1,0},{2,1},{3,2},{4,3},{5,4},{6,5},{7,6},{8,7},{9,8},{10,9},{11,1... | collective-permute-start | bytes 73736 | tf_op jit(solution)/shard_map/ppermute | solution.py:551
  28.6 0.8 %copy-start = (s32[256]{0:T(256)S(1)}, s32[256]{0:T(256)}, u32[]{:S(2)}) copy-start(s32[256]{0:T(256)} %seam.1) | copy-start | bytes 3076
  28.6 2.2 %collective-permute-start = (f32[1,128]{1,0:T(1,128)S(1)}, f32[1,128]{1,0:T(1,128)S(1)}, u32[]{:S(2)}, u32[]{:S(2)}) collective-permute-start(f32[1,128]{1,0:T(1,128)S(1)} %bitcast.4), channel_id=1, source_target_pairs={{16,17},{17,18},{18,19},{19,20},{20,21},{21,22},{22,23},{23,24},{2... | collective-permute-start | bytes 1544 | tf_op jit(solution)/shard_map/ppermute | solution.py:558

commit v7 on v6

--- a/solution.py
+++ b/solution.py
@@ -197,12 +197,13 @@
     class Block:
         def __init__(self, block, parts, basins):
             self.block, self.parts = block, parts
-            self.rows = pl.ds(pl.multiple_of(block * ROWS, ROWS), ROWS)
-            ahead = jnp.minimum(block + 1, blocks - 1) * ROWS
-            self.beyond = pl.ds(pl.multiple_of(ahead, ROWS), ROWS)
+            self.rows = pl.ds(block * ROWS, ROWS)
+            ahead = min(block + 1, blocks - 1) * ROWS
+            self.beyond = pl.ds(ahead, ROWS)
             own_depth = depth[self.rows, :].astype(jnp.float32)
             next_depth = depth[self.beyond, :][0:1].astype(jnp.float32)
-            next_depth = jnp.where(block == blocks - 1, 0.0, next_depth)
+            if block == blocks - 1:
+                next_depth = jnp.zeros_like(next_depth)
             self.face_depth = jnp.minimum(own_depth, northern(own_depth, next_depth))
             basin = label[self.rows, :]
             basins[...] = basin.astype(jnp.float32)
@@ -247,8 +248,9 @@
     def rows_of(parts, basins, block, fill):
         for pair in range(ROWS // 2):
             first = 2 * pair
-            for k in range(first * levels // ROWS, (first + 2) * levels // ROWS):
-                fill.level(k)
+            if fill is not None:
+                for k in range(first * levels // ROWS, (first + 2) * levels // ROWS):
+                    fill.level(k)
             spreads = [
                 lambda q, k, count, r=r: jnp.broadcast_to(parts[q, k, r : r + 1, :], (count, width))
                 for r in (first, first + 1)
@@ -259,31 +261,26 @@
             sums = products.pair(spreads, labels, levels)
             tile = class_tile(*sums)
             parcel[2 * block + pair // 2, 8 * (pair % 2) : 8 * (pair % 2) + 8, :] = tile
-        fill.close()
+        if fill is not None:
+            fill.close()
 
     for copy in planes[:3]:
         copy.wait()
     field_copy(0, 0).wait()
     field_copy(1, 0).wait()
-    opening = Block(jnp.int32(0), even, even_basins)
+    opening = Block(0, even, even_basins)
     for k in range(levels):
         opening.level(k)
     for copy in planes[3:]:
         copy.wait()
     opening.close()
 
-    def two_blocks(i, carry):
-        @pl.when(i < chunks - 1)
-        def _():
-            field_copy(0, i + 1).wait()
-            field_copy(1, i + 1).wait()
-
-        rows_of(even, even_basins, 2 * i, Block(2 * i + 1, odd, odd_basins))
-        ahead = jnp.minimum(2 * i + 2, blocks - 1)
-        rows_of(odd, odd_basins, 2 * i + 1, Block(ahead, even, even_basins))
-        return carry
-
-    lax.fori_loop(0, chunks, two_blocks, 0)
+    for block in range(blocks):
+        if block % 2 == 0 and block // 2 + 1 < chunks:
+            field_copy(0, block // 2 + 1).wait()
+            field_copy(1, block // 2 + 1).wait()
+        now, ahead = ((even, even_basins), (odd, odd_basins))[:: 1 if block % 2 == 0 else -1]
+        rows_of(*now, block, Block(block + 1, *ahead) if block + 1 < blocks else None)
 
     final = parallels - 1
     half = width // 2

time: 51.1 us -> 50.7 us (level)
  no operation moved by 1% of the time
where the time goes in v7:
time: 50.7 us; the launch traced here: 50.4 us
  blocking collectives  18.6 us (37%)
  Pallas kernels  14.4 us (28%)
  starting transfers between devices  9.88 us (19%)
  waiting for transfers between devices  6.56 us (13%)
  between operations  0.75 us (1%)
    all_to_all x1, blocking collectives, exchanged(): return lax.all_to_all(pieces, axis, split_axis=0, concat_axis=0, tiled=True)  18.6 us
    pallas_call x1, Pallas kernels, body(): pl.pallas_call(rows_kernel, in_specs=[anywhere, anywhere, in_smem] + [any...  11.8 us
    all_to_all x1, starting transfers between devices, exchanged(): return lax.all_to_all(pieces, axis, split_axis=0, concat_axis=0, tiled=True)  7.17 us
    all_to_all x1, waiting for transfers between devices, exchanged(): return lax.all_to_all(pieces, axis, split_axis=0, concat_axis=0, tiled=True)  6.55 us
    ppermute x1, starting transfers between devices, body(): lax.ppermute(southernmost, 'lat', [(i + 1, i) for i in range(lat_size - 1)])  1.92 us
    pallas_call x1, Pallas kernels, body(): pl.pallas_call(functools.partial(last_kernel, lon_size, lat_size), in_spe...  1.4 us
    pallas_call x1, Pallas kernels, body(): pl.pallas_call(functools.partial(finish_kernel, unit_scale, implied_scale...  1.2 us
  transfers between devices with their start and end apart: 3, of which 1 were waited for; matrix products, arithmetic and copies ran while one was open for 0% of the time, Pallas kernels for 3%

profile of v7, /device:TPU:32, one launch (start us, length us, event | category | flops | bytes accessed | tf_op | source)
XLA Modules:
  0.0 50.4 jit_solution(13816061764263764494)
XLA Ops:
  0.6 11.8 %rows.1 = (f32[16,32,128]{2,1,0:T(8,128)}, f32[56,256]{1,0:T(8,128)}, f32[24,256]{1,0:T(8,128)}) custom-call(f32[16,64,256]{2,1,0:T(8,128)} %theta_hbm.1, f32[16,64,256]{2,1,0:T(8,128)} %speed_hbm.1, f32[16]{0:T(128)} %tier.1, f32[64,256]{1,0:T(8,128)} %zonal_hbm.1, f32[64,256]{1,0:T(8,128)} %plan_hbm.1, f32[64,256]{1,0:T(8,128)} %energy_hbm.1, ...), custom_call_target="tpu_custom_call" | custom-call | flops 8000000000 | bytes 4000000 | tf_op jit(solution)/shard_map/rows/pallas_call | solution.py:509
  12.5 0.0 copy-start.2
  12.5 0.0 copy-start.1
  12.5 7.2 %all-to-all-start = ((f32[16,32,128]{2,1,0:T(8,128)}), f32[16,32,128]{2,1,0:T(8,128)S(1)}, u32[]{:S(2)}, u32[]{:S(2)}) async-start(f32[16,32,128]{2,1,0:T(8,128)} %get-tuple-element.11), calls=%async_computation | async-start | bytes 524288 | tf_op jit(solution)/shard_map/all_to_all | solution.py:479
  19.7 0.0 copy-done.2
  19.7 1.9 %collective-permute-start.1 = (f32[24,256]{1,0:T(8,128)S(1)}, f32[24,256]{1,0:T(8,128)S(1)}, u32[]{:S(2)}, u32[]{:S(2)}) collective-permute-start(f32[24,256]{1,0:T(8,128)S(1)} %copy-done.2), channel_id=1, source_target_pairs={{1,0},{2,1},{3,2},{4,3},{5,4},{6,5},{7,6},{8,7},{9,8},{10,9},{11,1... | collective-permute-start | bytes 73736 | tf_op jit(solution)/shard_map/ppermute | solution.py:548
  21.6 6.6 %all-to-all-done.parcels = f32[16,32,128]{2,1,0:T(8,128)S(1)} async-done(((f32[16,32,128]{2,1,0:T(8,128)}), f32[16,32,128]{2,1,0:T(8,128)S(1)}, u32[]{:S(2)}, u32[]{:S(2)}) %all-to-all-start) | async-done | bytes 262176 | tf_op jit(solution)/shard_map/all_to_all | solution.py:479
  28.2 0.0 copy-start
  28.2 0.8 %collective-permute-start = (f32[1,128]{1,0:T(1,128)S(1)}, f32[1,128]{1,0:T(1,128)S(1)}, u32[]{:S(2)}, u32[]{:S(2)}) collective-permute-start(f32[1,128]{1,0:T(1,128)S(1)} %bitcast.4), channel_id=1, source_target_pairs={{16,17},{17,18},{18,19},{19,20},{20,21},{21,22},{22,23},{23,24},{2... | collective-permute-start | bytes 1544 | tf_op jit(solution)/shard_map/ppermute | solution.py:555
  29.0 0.0 collective-permute-done.1.halo
  29.0 0.0 copy-done.1
  29.0 0.0 copy-done
  29.1 1.4 %last_row.1 = f32[24,128]{1,0:T(8,128)S(1)} custom-call(s32[256]{0:T(256)S(1)} %copy-done, f32[16,32,128]{2,1,0:T(8,128)S(1)} %all-to-all-done.parcels, f32[56,256]{1,0:T(8,128)S(1)} %copy-done.1, f32[24,256]{1,0:T(8,128)S(1)} %collective-permute-done.1.halo), custom_call_target="tpu_custom_call" | custom-call | flops 1000000000 | bytes 600000 | tf_op jit(solution)/shard_map/last_row/pallas_call | solution.py:556
  30.5 0.0 collective-permute-done
  30.5 0.1 and_select_fusion
  30.6 18.6 %all_to_all.10.shares = f32[16,24,128]{2,1,0:T(8,128)S(1)} all-to-all(f32[16,24,128]{2,1,0:T(8,128)S(1)} %broadcast_in_dim.19), channel_id=1, replica_groups=mesh['lon'=16,'lat'=16] {'lon'}, dimensions={0} | all-to-all | bytes 393216 | tf_op jit(solution)/shard_map/all_to_all | solution.py:479
  49.2 1.2 %finish.1 = (f32[4,64,128]{2,1,0:T(8,128)}, f32[4,16,64]{2,1,0:T(8,128)}, f32[4,64]{1,0:T(4,128)}, f32[4,64]{1,0:T(4,128)}) custom-call(f32[16,24,128]{2,1,0:T(8,128)S(1)} %all_to_all.10.shares), custom_call_target="tpu_custom_call" | custom-call | tf_op jit(solution)/shard_map/finish/pallas_call | solution.py:574
  (4 shorter events, 0.1 us)
Async XLA Ops:
  12.5 7.2 %copy-start.2 = (f32[24,256]{1,0:T(8,128)S(1)}, f32[24,256]{1,0:T(8,128)}, u32[]{:S(2)}) copy-start(f32[24,256]{1,0:T(8,128)} %get-tuple-element.13) | copy-start | bytes 73732
  12.5 16.6 %copy-start.1 = (f32[56,256]{1,0:T(8,128)S(1)}, f32[56,256]{1,0:T(8,128)}, u32[]{:S(2)}) copy-start(f32[56,256]{1,0:T(8,128)} %get-tuple-element.12.last) | copy-start | bytes 172036
  12.5 15.7 %all-to-all-start = ((f32[16,32,128]{2,1,0:T(8,128)}), f32[16,32,128]{2,1,0:T(8,128)S(1)}, u32[]{:S(2)}, u32[]{:S(2)}) async-start(f32[16,32,128]{2,1,0:T(8,128)} %get-tuple-element.11), calls=%async_computation | async-start | bytes 524288 | tf_op jit(solution)/shard_map/all_to_all | solution.py:479
  19.7 9.3 %collective-permute-start.1 = (f32[24,256]{1,0:T(8,128)S(1)}, f32[24,256]{1,0:T(8,128)S(1)}, u32[]{:S(2)}, u32[]{:S(2)}) collective-permute-start(f32[24,256]{1,0:T(8,128)S(1)} %copy-done.2), channel_id=1, source_target_pairs={{1,0},{2,1},{3,2},{4,3},{5,4},{6,5},{7,6},{8,7},{9,8},{10,9},{11,1... | collective-permute-start | bytes 73736 | tf_op jit(solution)/shard_map/ppermute | solution.py:548
  28.2 0.8 %copy-start = (s32[256]{0:T(256)S(1)}, s32[256]{0:T(256)}, u32[]{:S(2)}) copy-start(s32[256]{0:T(256)} %seam.1) | copy-start | bytes 3076
  28.2 2.2 %collective-permute-start = (f32[1,128]{1,0:T(1,128)S(1)}, f32[1,128]{1,0:T(1,128)S(1)}, u32[]{:S(2)}, u32[]{:S(2)}) collective-permute-start(f32[1,128]{1,0:T(1,128)S(1)} %bitcast.4), channel_id=1, source_target_pairs={{16,17},{17,18},{18,19},{19,20},{20,21},{21,22},{22,23},{23,24},{2... | collective-permute-start | bytes 1544 | tf_op jit(solution)/shard_map/ppermute | solution.py:555
